TPU v7x, 8 devices: a whole 2x2x1 slice. The times are simulated.
8 devices in a mesh: rep: 1 (over z), r: 2 (over y), s: 4 (over x, core).
Axes of the slice: x: 2, y: 2, z: 1, core: 2. Of those that a mesh axis runs over, the one named last changes fastest.
Arguments:
- x: bfloat16 [8, 4096, 896], P(('rep', 'r', 's'))
- dy: bfloat16 [8, 4096, 896], P(('rep', 'r', 's'))
- w_gate: bfloat16 [2, 896, 2560], P(None, 's')
- w_up: bfloat16 [2, 896, 2560], P(None, 's')
- w_down: bfloat16 [2, 2560, 896], P(None, 's')
Outputs:
- output 1: bfloat16 [8, 4096, 896], P(('rep', 'r', 's'))
- output 2: bfloat16 [2, 896, 2560], P('rep', 's')
- output 3: bfloat16 [2, 896, 2560], P('rep', 's')
- output 4: bfloat16 [2, 2560, 896], P('rep', 's')
All inputs are finite; a program needn't handle non-finite values.
Results may differ from a plain program's by a relative error of at most 0.018.
Values are sent between devices in bfloat16 or wider.
A program may use at most 2 GiB of HBM per device.

v0:
```python
import jax
import jax.numpy as jnp
from jax import lax
from jax.sharding import PartitionSpec as P

NAMES = ("w_gate", "w_up", "w_down")


def matmul(a, w):
    return jnp.dot(a, w, preferred_element_type=jnp.float32).astype(jnp.bfloat16)


def normed(h):
    wide = h.astype(jnp.float32)
    scale = lax.rsqrt(jnp.mean(wide**2, -1, keepdims=True) + 1e-6)
    return (wide * scale).astype(jnp.bfloat16)


def layer(h, w):
    a = normed(h)
    gate = jnp.dot(a, w["w_gate"], preferred_element_type=jnp.float32)
    up = jnp.dot(a, w["w_up"], preferred_element_type=jnp.float32)
    return h + matmul((jax.nn.silu(gate) * up).astype(jnp.bfloat16), w["w_down"])


def solution(mesh):
    def fetched(weights, number):
        return {name: lax.all_gather(w[number], "s", axis=0, tiled=True) for name, w in zip(NAMES, weights, strict=True)}

    def summed(term):
        return lax.psum(lax.psum_scatter(term, "s", scatter_dimension=0, tiled=True), "r")

    def step(x, dy, *weights):
        layers = weights[0].shape[0]
        h, inputs = x[0], []
        for number in range(layers):
            inputs.append(h)
            h = layer(h, fetched(weights, number))
        by_h, mine = dy[0], [None] * layers
        for number in reversed(range(layers)):
            _, back = jax.vjp(lambda w, h: layer(h, w), fetched(weights, number), inputs[number])
            by_w, by_h = back(by_h)
            mine[number] = [summed(by_w[name]) for name in NAMES]
        return (by_h[None], *(jnp.stack([mine[number][i] for number in range(layers)]) for i in range(3)))

    states, cut = P(("rep", "r", "s"), None, None), P(None, "s", None)
    return jax.shard_map(
        step,
        mesh=mesh,
        in_specs=(states, states) + (cut,) * 3,
        out_specs=(states,) + (P("rep", "s", None),) * 3,
        check_vma=False,
    )
```

profile of v0, /device:TPU:0, one launch (start us, length us, event | category | flops | bytes accessed | tf_op | source)
XLA Modules:
  0.0 857.3 jit_solution(9401729165000621826)
XLA Ops:
  7.2 3.1 fusion.65
  10.4 0.0 all-gather.15.cloned.1.call-start
  10.4 3.1 fusion.64
  13.6 0.0 all-gather.17.cloned.1.call-start
  13.6 3.2 fusion.63
  16.9 0.5 all-gather.23.cloned.1.call-update
  17.5 0.5 all-gather.21.cloned.1.call-update
  18.0 0.5 all-gather.19.cloned.1.call-update
  18.6 10.8 %copy.10 = bf16[1,4096,896]{1,2,0:T(8,128)(2,1)} copy(bf16[1,4096,896]{2,1,0:T(8,128)(2,1)} %param.5) | data formatting | bytes 14680064 | tf_op args[0]
  29.4 4.6 fusion.15
  34.0 0.6 copy-done.1
  34.6 10.8 %copy.9 = bf16[1,4096,896]{1,2,0:T(8,128)(2,1)} copy(bf16[1,4096,896]{2,1,0:T(8,128)(2,1)} %param.6) | data formatting | bytes 14680064 | tf_op args[1]
  45.4 1.8 all-gather.13.cloned.1.call-done
  47.1 29.5 %fusion.41 = f32[4096,2560]{1,0:T(8,128)} fusion(bf16[1,4096,896]{1,2,0:T(8,128)(2,1)} %copy.10, f32[4096]{0:T(1024)S(1)} %fusion.56, bf16[1,896,2560]{2,1,0:T(8,128)(2,1)} %all-gather.13.cloned.1.call-done), kind=kOutput, calls=%fused_computation.60 | convolution fusion | flops 18801491968 | bytes 53886976 | tf_op jit(solution)/shard_map/dot_general | solution.py:21
  76.6 5.9 all-gather.15.cloned.1.call-done
  82.5 49.8 %multiply_convert_fusion.1 = (bf16[4096,2560]{1,0:T(8,128)(2,1)}, f32[4096,2560]{1,0:T(8,128)}) fusion(f32[4096,2560]{1,0:T(8,128)} %fusion.41, bf16[1,896,2560]{2,1,0:T(8,128)(2,1)} %all-gather.15.cloned.1.call-done, bf16[1,4096,896]{1,2,0:T(8,128)(2,1)} %copy.10, f32[4096]{0:T(1024)S(1)} %fusion.56), kind=kOutput, calls=%fused_computation.13 | convolution fusion | flops 18864406528 | bytes 116801536 | tf_op jit(solution)/shard_map/dot_general | solution.py:22
  132.3 26.8 %fusion.18 = (f32[4096]{0:T(1024)S(1)}, bf16[4096,896]{0,1:T(8,128)(2,1)}) fusion(bf16[4096,2560]{1,0:T(8,128)(2,1)} %get-tuple-element.20, bf16[1,2560,896]{2,1,0:T(8,128)(2,1)} %all-gather.17.cloned.1.call-done, bf16[1,4096,896]{1,2,0:T(8,128)(2,1)} %copy.10), kind=kOutput, calls=%fused_computation.40 | convolution fusion | flops 18808827904 | bytes 40255488 | tf_op jit(solution)/shard_map/dot_general | solution.py:10
  159.1 0.6 copy-done.7
  159.8 29.6 %fusion.33 = f32[4096,2560]{1,0:T(8,128)} fusion(bf16[4096,896]{0,1:T(8,128)(2,1)} %get-tuple-element.23, f32[4096]{0:T(1024)S(1)} %fusion.57, bf16[1,896,2560]{2,1,0:T(8,128)(2,1)} %all-gather.23.cloned.1.call-done), kind=kOutput, calls=%fused_computation.57 | convolution fusion | flops 18801491968 | bytes 53886976 | tf_op jit(solution)/shard_map/jvp()/dot_general | solution.py:22
  189.4 28.4 %convolution_convert_fusion.1 = bf16[4096,2560]{1,0:T(8,128)(2,1)} fusion(bf16[1,4096,896]{2,1,0:T(8,128)(2,1)} %param.6, bf16[1,2560,896]{2,1,0:T(8,128)(2,1)} %all-gather.21.cloned.1.call-done), kind=kOutput, calls=%fused_computation.29 | convolution fusion | flops 18800967680 | bytes 32899072 | tf_op jit(solution)/shard_map/transpose(jvp())/dot_general | solution.py:10
  217.9 6.6 all-gather.19.cloned.1.call-done
  224.5 58.4 %fusion.1 = (bf16[4096,2560]{1,0:T(8,128)(2,1)}, f32[4096,2560]{1,0:T(8,128)}) fusion(f32[4096,2560]{1,0:T(8,128)} %fusion.33, bf16[4096,2560]{1,0:T(8,128)(2,1)} %convolution_convert_fusion.1, bf16[1,896,2560]{2,1,0:T(8,128)(2,1)} %all-gather.19.cloned.1.call-done, bf16[4096,896]{0,1:T(8,128)(2,1)} %get-tuple-element.23, f32[4096]{0:T(1024)S(1)} %fusion.57), kind=kOutput, calls=%fused_computation.7 | convolution fusion | flops 18927321088 | bytes 137773056 | tf_op jit(solution)/shard_map/jvp()/dot_general | solution.py:21
  282.9 23.6 %fusion.46 = bf16[4096,896]{0,1:T(8,128)(2,1)} fusion(bf16[4096,2560]{1,0:T(8,128)(2,1)} %get-tuple-element.24, bf16[1,896,2560]{2,1,0:T(8,128)(2,1)S(1)} %copy-done.9), kind=kOutput, calls=%fused_computation.64 | convolution fusion | flops 18790481920 | bytes 32899072 | tf_op jit(solution)/shard_map/transpose(jvp())/dot_general | solution.py:21
  306.5 38.2 %fusion.20 = (f32[4096]{0:T(1024)S(1)}, bf16[4096,896]{0,1:T(8,128)(2,1)}) fusion(bf16[4096,896]{0,1:T(8,128)(2,1)} %get-tuple-element.23, bf16[4096,896]{0,1:T(8,128)(2,1)} %fusion.46, bf16[1,896,2560]{2,1,0:T(8,128)(2,1)} %all-gather.23.cloned.1.call-done, bf16[4096,2560]{1,0:T(8,128)(2,1)} %convolution_convert_fusion.1, f32[4096,2560]{1,0:T(8,128)} %get-tuple-element.25), kind=kOutput, calls=%fused_computation.42 | convolution fusion | flops 18875412480 | bytes 89538560 | tf_op jit(solution)/shard_map/transpose(jvp())/dot_general | solution.py:22
  344.8 9.8 %fusion.23 = bf16[4096,896]{0,1:T(8,128)(2,1)S(1)} fusion(bf16[4096,896]{0,1:T(8,128)(2,1)} %get-tuple-element.23, bf16[4096,896]{0,1:T(8,128)(2,1)} %get-tuple-element.27, bf16[1,4096,896]{1,2,0:T(8,128)(2,1)} %copy.9, f32[4096]{0:T(1024)S(1)} %multiply_multiply_fusion.1, f32[4096]{0:T(1024)S(1)} %fusion.57), kind=kLoop, calls=%fused_computation.45 | loop fusion | flops 25690112 | bytes 29392896 | tf_op jit(solution)/shard_map/transpose(jvp())/add_any | solution.py:14
  354.6 2.9 copy-done
  357.5 26.4 %convolution_convert_fusion.2 = bf16[2560,896]{1,0:T(8,128)(2,1)} fusion(bf16[4096,2560]{1,0:T(8,128)(2,1)} %get-tuple-element.20, bf16[4096,896]{0,1:T(8,128)(2,1)S(1)} %fusion.23), kind=kOutput, calls=%fused_computation.54 | convolution fusion | flops 18792775680 | bytes 32899072 | tf_op jit(solution)/shard_map/transpose(jvp())/dot_general | solution.py:10
  384.0 0.0 reduce-scatter.17.cloned.1.call-start
  384.0 36.3 %fusion.26 = bf16[2560,896]{1,0:T(8,128)(2,1)} fusion(bf16[1,4096,896]{2,1,0:T(8,128)(2,1)} %param.6, f32[4096,2560]{1,0:T(8,128)} %fusion.33, f32[4096,2560]{1,0:T(8,128)} %get-tuple-element.25), kind=kOutput, calls=%fused_computation.51 | convolution fusion | flops 18855690240 | bytes 95813632 | tf_op jit(solution)/shard_map/transpose(jvp())/dot_general | solution.py:10
  420.3 0.0 reduce-scatter.11.cloned.1.call-start
  420.4 54.4 %fusion.3 = (bf16[4096,2560]{1,0:T(8,128)(2,1)}, bf16[4096,2560]{1,0:T(8,128)(2,1)}) fusion(f32[4096,2560]{1,0:T(8,128)} %fusion.41, f32[4096,2560]{1,0:T(8,128)} %get-tuple-element.21, bf16[4096,896]{0,1:T(8,128)(2,1)} %copy-done, bf16[1,2560,896]{2,1,0:T(8,128)(2,1)} %all-gather.17.cloned.1.call-done), kind=kOutput, calls=%fused_computation.9 | convolution fusion | flops 18926796800 | bytes 137756672 | tf_op jit(solution)/shard_map/transpose(jvp())/dot_general | solution.py:10
  474.8 34.1 %fusion.29 = bf16[896,2560]{1,0:T(8,128)(2,1)} fusion(bf16[4096,2560]{1,0:T(8,128)(2,1)} %get-tuple-element.29, bf16[1,4096,896]{1,2,0:T(8,128)(2,1)} %copy.10, f32[4096]{0:T(1024)S(1)} %copy-done.4, f32[4096,2560]{1,0:T(8,128)} %fusion.41), kind=kOutput, calls=%fused_computation.52 | convolution fusion | flops 18866700288 | bytes 74858496 | tf_op jit(solution)/shard_map/transpose(jvp())/dot_general | solution.py:22
  508.9 0.0 reduce-scatter.13.cloned.1.call-start
  509.0 34.1 %fusion.30 = bf16[896,2560]{1,0:T(8,128)(2,1)} fusion(bf16[4096,2560]{1,0:T(8,128)(2,1)} %convolution_convert_fusion.1, bf16[4096,896]{0,1:T(8,128)(2,1)} %get-tuple-element.23, f32[4096]{0:T(1024)S(1)} %copy-done.6, f32[4096,2560]{1,0:T(8,128)} %get-tuple-element.25), kind=kOutput, calls=%fused_computation.53 | convolution fusion | flops 18866700288 | bytes 74858496 | tf_op jit(solution)/shard_map/transpose(jvp())/dot_general | solution.py:22
  543.1 0.0 reduce-scatter.9.cloned.1.call-start
  543.2 25.2 %convolution_convert_fusion.3 = bf16[896,2560]{1,0:T(8,128)(2,1)} fusion(bf16[4096,2560]{1,0:T(8,128)(2,1)} %get-tuple-element.24, bf16[4096,896]{0,1:T(8,128)(2,1)} %get-tuple-element.23, f32[4096]{0:T(1024)S(1)} %copy-done.6), kind=kOutput, calls=%fused_computation.55 | convolution fusion | flops 18801491968 | bytes 32915456 | tf_op jit(solution)/shard_map/transpose(jvp())/dot_general | solution.py:21
  568.4 0.0 reduce-scatter.7.cloned.1.call-start
  568.5 25.1 %convolution_convert_fusion.4 = bf16[896,2560]{1,0:T(8,128)(2,1)} fusion(bf16[4096,2560]{1,0:T(8,128)(2,1)} %get-tuple-element.28, bf16[1,4096,896]{1,2,0:T(8,128)(2,1)} %copy.10, f32[4096]{0:T(1024)S(1)} %copy-done.4), kind=kOutput, calls=%fused_computation.56 | convolution fusion | flops 18801491968 | bytes 32915456 | tf_op jit(solution)/shard_map/transpose(jvp())/dot_general | solution.py:21
  593.6 0.0 all-reduce.3.cloned.1.call-start
  593.7 25.1 %fusion.53 = bf16[4096,896]{0,1:T(8,128)(2,1)} fusion(bf16[4096,2560]{1,0:T(8,128)(2,1)} %get-tuple-element.28, bf16[1,896,2560]{2,1,0:T(8,128)(2,1)} %all-gather.13.cloned.1.call-done), kind=kOutput, calls=%fused_computation.71 | convolution fusion | flops 18790481920 | bytes 32899072 | tf_op jit(solution)/shard_map/transpose(jvp())/dot_general | solution.py:21
  618.8 17.4 %reduce-scatter.9.cloned.1.call-done = bf16[224,2560]{1,0:T(8,128)(2,1)} async-done(((bf16[896,2560]{1,0:T(8,128)(2,1)}), bf16[224,2560]{1,0:T(8,128)(2,1)}) %reduce-scatter.9.cloned.1.call-update) | async-done | bytes 1146896 | tf_op jit(solution)/shard_map/reduce_scatter | solution.py:31
  636.2 43.1 %reduce-scatter.7.cloned.1.call-done = bf16[224,2560]{1,0:T(8,128)(2,1)} async-done(((bf16[896,2560]{1,0:T(8,128)(2,1)}), bf16[224,2560]{1,0:T(8,128)(2,1)}) %reduce-scatter.7.cloned.1.call-update) | async-done | bytes 1146896 | tf_op jit(solution)/shard_map/reduce_scatter | solution.py:31
  679.4 38.1 %fusion.17 = (f32[4096]{0:T(1024)S(1)}, bf16[4096,896]{0,1:T(8,128)(2,1)}) fusion(bf16[1,4096,896]{1,2,0:T(8,128)(2,1)} %copy.10, bf16[4096,896]{0,1:T(8,128)(2,1)} %fusion.53, bf16[1,896,2560]{2,1,0:T(8,128)(2,1)} %all-gather.15.cloned.1.call-done, bf16[4096,2560]{1,0:T(8,128)(2,1)} %get-tuple-element.29, f32[4096,2560]{1,0:T(8,128)} %fusion.41), kind=kOutput, calls=%fused_computation.39 | convolution fusion | flops 18875412480 | bytes 89538560 | tf_op jit(solution)/shard_map/transpose(jvp())/dot_general | solution.py:22
  717.5 12.4 %fusion.22 = bf16[1,4096,896]{1,2,0:T(8,128)(2,1)} fusion(bf16[4096,896]{0,1:T(8,128)(2,1)} %copy-done, bf16[4096,896]{0,1:T(8,128)(2,1)} %get-tuple-element.31, bf16[1,4096,896]{1,2,0:T(8,128)(2,1)} %copy.10, f32[4096]{0:T(1024)S(1)} %multiply_multiply_fusion, f32[4096]{0:T(1024)S(1)} %copy-done.4), kind=kLoop, calls=%fused_computation.44 | loop fusion | flops 25690112 | bytes 29392896 | tf_op jit(solution)/shard_map/broadcast_in_dim | solution.py:44
  729.9 10.8 %copy.11 = bf16[1,4096,896]{2,1,0:T(8,128)(2,1)} copy(bf16[1,4096,896]{1,2,0:T(8,128)(2,1)} %fusion.22) | data formatting | bytes 14680064
  740.7 101.8 %all-reduce.3.cloned.1.call-done = (bf16[1,224,2560]{2,1,0:T(8,128)(2,1)}, bf16[1,224,2560]{2,1,0:T(8,128)(2,1)}, bf16[1,224,2560]{2,1,0:T(8,128)(2,1)}, bf16[1,...) async-done(((bf16[1,224,2560]{2,1,0:T(8,128)(2,1)}, bf16[1,224,2560]{2,1,0:T(8,128)(2,1)}, bf16[1,224,2560]{2,1,0:T(8,128)(2,1)}, ...) | async-done | bytes 6881296 | tf_op jit(solution)/shard_map/psum | solution.py:31
  842.5 3.2 pad_maximum_fusion.2
  845.7 4.8 pad_maximum_fusion
  (43 shorter events, 0.5 us)
Async XLA Ops:
  7.2 40.0 %all-gather.13.cloned.1.call-start = ((), (), s32[]{:S(2)}) async-start(), calls=%async_computation.12 | async-start | bytes 5734400 | tf_op jit(solution)/shard_map/all_gather | solution.py:28
  10.4 72.1 %all-gather.15.cloned.1.call-start = ((), (), s32[]{:S(2)}) async-start(), calls=%async_computation.13 | async-start | bytes 5734400 | tf_op jit(solution)/shard_map/all_gather | solution.py:28
  13.6 118.7 %all-gather.17.cloned.1.call-start = ((), (), s32[]{:S(2)}) async-start(), calls=%async_computation.14 | async-start | bytes 5734400 | tf_op jit(solution)/shard_map/all_gather | solution.py:28
  16.8 143.0 %all-gather.23.cloned.1.call-start = ((), (), s32[]{:S(2)}) async-start(), calls=%async_computation.17 | async-start | bytes 5734400 | tf_op jit(solution)/shard_map/all_gather | solution.py:28
  17.4 172.0 %all-gather.21.cloned.1.call-start = ((), (), s32[]{:S(2)}) async-start(), calls=%async_computation.16 | async-start | bytes 5734400 | tf_op jit(solution)/shard_map/all_gather | solution.py:28
  18.0 206.5 %all-gather.19.cloned.1.call-start = ((), (), s32[]{:S(2)}) async-start(), calls=%async_computation.15 | async-start | bytes 5734400 | tf_op jit(solution)/shard_map/all_gather | solution.py:28
  18.6 600.2 %reduce-scatter.15.cloned.1.call-start = ((), (), s32[]{:S(2)}) async-start(), calls=%async_computation.10 | async-start | bytes 5734400 | tf_op jit(solution)/shard_map/reduce_scatter | solution.py:31
  34.0 0.6 copy-start.1
  34.6 47.9 %copy-start.3 = (f32[4096]{0:T(1024)}, f32[4096]{0:T(1024)S(1)}, u32[]{:S(2)}) copy-start(f32[4096]{0:T(1024)S(1)} %fusion.56) | copy-start | bytes 49156
  159.1 0.6 copy-start.7
  159.8 185.0 %copy-start.5 = (f32[4096]{0:T(1024)}, f32[4096]{0:T(1024)S(1)}, u32[]{:S(2)}) copy-start(f32[4096]{0:T(1024)S(1)} %fusion.57) | copy-start | bytes 49156
  224.5 58.4 %copy-start.9 = (bf16[1,896,2560]{2,1,0:T(8,128)(2,1)S(1)}, bf16[1,896,2560]{2,1,0:T(8,128)(2,1)}, u32[]{:S(2)}) copy-start(bf16[1,896,2560]{2,1,0:T(8,128)(2,1)} %all-gather.19.cloned.1.call-done) | copy-start | bytes 13762564
  306.5 38.3 %copy-start.8 = (f32[4096]{0:T(1024)S(1)}, f32[4096]{0:T(1024)}, u32[]{:S(2)}) copy-start(f32[4096]{0:T(1024)} %copy-done.7) | copy-start | bytes 49156
  354.6 3.0 copy-start
  384.0 234.8 %reduce-scatter.17.cloned.1.call-start = ((), (), s32[]{:S(2)}) async-start(), calls=%async_computation.11 | async-start | bytes 5734400 | tf_op jit(solution)/shard_map/reduce_scatter | solution.py:31
  420.3 198.5 %reduce-scatter.11.cloned.1.call-start = ((), (), s32[]{:S(2)}) async-start(), calls=%async_computation.8 | async-start | bytes 5734400 | tf_op jit(solution)/shard_map/reduce_scatter | solution.py:31
  420.4 54.4 %copy-start.4 = (f32[4096]{0:T(1024)S(1)}, f32[4096]{0:T(1024)}, u32[]{:S(2)}) copy-start(f32[4096]{0:T(1024)} %copy-done.3) | copy-start | bytes 49156
  474.8 34.2 %copy-start.6 = (f32[4096]{0:T(1024)S(1)}, f32[4096]{0:T(1024)}, u32[]{:S(2)}) copy-start(f32[4096]{0:T(1024)} %copy-done.5) | copy-start | bytes 49156
  508.9 109.9 %reduce-scatter.13.cloned.1.call-start = ((), (), s32[]{:S(2)}) async-start(), calls=%async_computation.9 | async-start | bytes 5734400 | tf_op jit(solution)/shard_map/reduce_scatter | solution.py:31
  543.1 93.1 %reduce-scatter.9.cloned.1.call-start = ((), (), s32[]{:S(2)}) async-start(), calls=%async_computation.7 | async-start | bytes 5734400 | tf_op jit(solution)/shard_map/reduce_scatter | solution.py:31
  568.4 110.9 %reduce-scatter.7.cloned.1.call-start = ((), (), s32[]{:S(2)}) async-start(), calls=%async_computation.6 | async-start | bytes 5734400 | tf_op jit(solution)/shard_map/reduce_scatter | solution.py:31
  593.6 248.9 %all-reduce.3.cloned.1.call-start = ((), (), s32[]{:S(2)}) async-start(), calls=%async_computation.18 | async-start | bytes 13762560 | tf_op jit(solution)/shard_map/psum | solution.py:31
  679.4 38.1 %copy-start.2 = (f32[4096]{0:T(1024)S(1)}, f32[4096]{0:T(1024)}, u32[]{:S(2)}) copy-start(f32[4096]{0:T(1024)} %copy-done.1) | copy-start | bytes 49156
Sparse Core Ops, SparseCore 0:
  10.5 36.5 all-gather.12
  48.7 33.7 all-gather.14
  84.0 33.7 all-gather.16
  119.8 33.7 all-gather.22
  154.9 33.7 all-gather.20
  190.7 33.7 all-gather.18
  384.1 40.7 reduce-scatter.14
  427.4 40.7 reduce-scatter.16
  509.0 40.7 reduce-scatter.10
  552.2 40.7 reduce-scatter.12
  595.4 40.7 reduce-scatter.8
  638.6 40.7 reduce-scatter.6
  682.3 160.1 all-reduce.2
where the time goes:
time: 864 us; the launch traced here: 857 us
  matrix products  583 us (67%)
  waiting for transfers between devices  178 us (21%)
  local copies, waits for them, and re-layouts  46 us (5%)
  other arithmetic  34.9 us (4%)
  between operations  14.2 us (2%)
    dot_general x6, matrix products, layer(): up = jnp.dot(a, w['w_up'], preferred_element_type=jnp.float32)  224 us
    dot_general x6, matrix products, layer(): gate = jnp.dot(a, w['w_gate'], preferred_element_type=jnp.float32)  187 us
    dot_general x5, matrix products, matmul(): jnp.dot(a, w, preferred_element_type=jnp.float32).astype(jnp.bfloat16)  172 us
    psum x1, waiting for transfers between devices, summed(): lax.psum(lax.psum_scatter(term, 's', scatter_dimension=0, tiled=True), 'r')  102 us
    reduce_scatter x6, waiting for transfers between devices, summed(): lax.psum_scatter(term, 's', scatter_dimension=0, tiled=True)  60.6 us
    unnamed x23, local copies, waits for them, and re-layouts  36.5 us
  transfers between devices with their start and end apart: 13, of which 6 were waited for; matrix products, arithmetic and copies ran while one was open for 57% of the time, Pallas kernels for 0%

commit v1 on v0

v1 whole, which is shorter than its diff:
```python
import functools

import jax
import jax.numpy as jnp
from jax import lax
from jax.experimental import pallas as pl
from jax.experimental.pallas import tpu as pltpu
from jax.sharding import PartitionSpec as P

F32, BF16 = jnp.float32, jnp.bfloat16
ANY = pl.BlockSpec(memory_space=pl.ANY)
TILE = 512
CHUNK = 1024
SUB = 512
EDGE = 256
EPS = 1e-6


def dot(a, b, over=(1, 0)):
    return lax.dot_general(a, b, (((over[0],), (over[1],)), ((), ())), preferred_element_type=F32)


def at(step, size):
    return pl.ds(pl.multiple_of(step * size, size), size)


def scale_of(h):
    return lax.rsqrt(jnp.mean(h * h, 0, keepdims=True) + EPS)


def turned(source, stage, sems, write):
    chunks = source.shape[0] // EDGE

    def copy(c, slot):
        return pltpu.make_async_copy(source.at[at(c, EDGE), :], stage.at[slot], sems.at[slot])

    copy(0, 0).start()
    copy(1, 1).start()

    def step(c, _):
        for slot in range(2):
            copy(2 * c + slot, slot).wait()
            write(2 * c + slot, stage[slot].T)

            @pl.when(2 * c + slot + 2 < chunks)
            def _():
                copy(2 * c + slot + 2, slot).start()
        return 0

    lax.fori_loop(0, chunks // 2, step, 0)


def forward_kernel(x, wg, wu, wd, xt_out, at_out, ht_out, at1_out, xt, a, total, p, stage, sems, osems):
    n, passes = pl.program_id(0), pl.num_programs(0)
    chunks = a.shape[1] // CHUNK

    @pl.when(n == 0)
    def _():
        def write(c, ht):
            h = ht.astype(F32)
            xt[:, at(c, EDGE)] = ht
            a[:, at(c, EDGE)] = (h * scale_of(h)).astype(BF16)

        turned(x, stage, sems, write)
        pltpu.make_async_copy(xt, xt_out, osems.at[0]).start()
        pltpu.make_async_copy(a, at_out, osems.at[1]).start()
        total[...] = jnp.zeros_like(total)

    def step(c, _):
        for i in range(CHUNK // SUB):
            tokens = pl.ds(pl.multiple_of(c * CHUNK + i * SUB, SUB), SUB)
            g, u = dot(wg[...], a[:, tokens], (0, 0)), dot(wu[...], a[:, tokens], (0, 0))
            p[:, pl.ds(i * SUB, SUB)] = (g * jax.nn.sigmoid(g) * u).astype(BF16)
        total[:, at(c, CHUNK)] += dot(wd[...], p[...], (0, 0))
        return 0

    lax.fori_loop(0, chunks, step, 0)

    @pl.when(n == passes - 1)
    def _():
        pltpu.make_async_copy(xt, xt_out, osems.at[0]).wait()
        pltpu.make_async_copy(a, at_out, osems.at[1]).wait()

        def last(c, _):
            cols = at(c, EDGE)
            h = (xt[:, cols].astype(F32) + total[:, cols].astype(BF16).astype(F32)).astype(BF16)
            xt[:, cols] = h
            h = h.astype(F32)
            a[:, cols] = (h * scale_of(h)).astype(BF16)
            return 0

        lax.fori_loop(0, a.shape[1] // EDGE, last, 0)
        one = pltpu.make_async_copy(xt, ht_out, osems.at[0])
        two = pltpu.make_async_copy(a, at1_out, osems.at[1])
        one.start(), two.start(), one.wait(), two.wait()


def forward(x, wg, wu, wd):
    tokens, d = x.shape
    state = jax.ShapeDtypeStruct((d, tokens), BF16)
    return pl.pallas_call(
        forward_kernel,
        grid=(wg.shape[1] // TILE,),
        in_specs=[ANY, pl.BlockSpec((d, TILE), lambda n: (0, n)), pl.BlockSpec((d, TILE), lambda n: (0, n)), pl.BlockSpec((TILE, d), lambda n: (n, 0))],
        out_specs=[ANY] * 4,
        out_shape=[state] * 4,
        scratch_shapes=[
            pltpu.VMEM((d, tokens), BF16),
            pltpu.VMEM((d, tokens), BF16),
            pltpu.VMEM((d, tokens), F32),
            pltpu.VMEM((TILE, CHUNK), BF16),
            pltpu.VMEM((2, EDGE, d), BF16),
            pltpu.SemaphoreType.DMA((2,)),
            pltpu.SemaphoreType.DMA((2,)),
        ],
        compiler_params=pltpu.CompilerParams(vmem_limit_bytes=63 * 2**20, dimension_semantics=("arbitrary",)),
        cost_estimate=pl.CostEstimate(flops=6 * tokens * d * wg.shape[1], bytes_accessed=60 * 2**20, transcendentals=0),
        name="forward_layer",
    )(x, wg, wu, wd)


def backward_kernel(turn_in, turn_out, at_in, ht_in, by_in, wg, wu, wd, og, ou, od, by_out, a, by, total, accg, accu, accd, p, dg, du, stage, sems, osems):
    n, passes = pl.program_id(0), pl.num_programs(0)
    chunks = a.shape[1] // CHUNK

    @pl.when(n == 0)
    def _():
        one = pltpu.make_async_copy(at_in, a, osems.at[0])
        one.start()
        if turn_in:
            def write(c, t):
                by[:, at(c, EDGE)] = t

            turned(by_in, stage, sems, write)
        else:
            two = pltpu.make_async_copy(by_in, by, osems.at[1])
            two.start()
            two.wait()
        total[...] = jnp.zeros_like(total)
        one.wait()

    accg[...] = jnp.zeros_like(accg)
    accu[...] = jnp.zeros_like(accu)
    accd[...] = jnp.zeros_like(accd)

    def step(c, _):
        cols = at(c, CHUNK)
        for i in range(CHUNK // SUB):
            tokens, q = pl.ds(pl.multiple_of(c * CHUNK + i * SUB, SUB), SUB), pl.ds(i * SUB, SUB)
            g, u = dot(wg[...], a[:, tokens], (0, 0)), dot(wu[...], a[:, tokens], (0, 0))
            dp = dot(wd[...], by[:, tokens]).astype(BF16).astype(F32)
            sg = jax.nn.sigmoid(g)
            s = g * sg
            p[:, q] = (s * u).astype(BF16)
            du[:, q] = (dp * s).astype(BF16)
            dg[:, q] = (dp * u * (sg + s * (1 - sg))).astype(BF16)
        total[:, cols] += dot(wg[...], dg[...]) + dot(wu[...], du[...])
        accg[...] += dot(a[:, cols], dg[...], (1, 1))
        accu[...] += dot(a[:, cols], du[...], (1, 1))
        accd[...] += dot(by[:, cols], p[...], (1, 1))
        return 0

    lax.fori_loop(0, chunks, step, 0)
    og[...] = accg[...].astype(BF16)
    ou[...] = accu[...].astype(BF16)
    od[...] = accd[...].T.astype(BF16)

    @pl.when(n == passes - 1)
    def _():
        one = pltpu.make_async_copy(ht_in, a, osems.at[0])
        one.start()
        one.wait()

        def changed(cols):
            da, h = total[:, cols].astype(BF16).astype(F32), a[:, cols].astype(F32)
            f = scale_of(h)
            dh = (f * da - h * (f * f * f * jnp.mean(da * h, 0, keepdims=True))).astype(BF16)
            return (by[:, cols].astype(F32) + dh.astype(F32)).astype(BF16)

        if turn_out:
            def copy(c, slot):
                return pltpu.make_async_copy(stage.at[slot], by_out.at[at(c, EDGE), :], sems.at[slot])

            def last(c, _):
                for slot in range(2):
                    @pl.when(c > 0)
                    def _():
                        copy(2 * c + slot - 2, slot).wait()

                    stage[slot] = changed(at(2 * c + slot, EDGE)).T
                    copy(2 * c + slot, slot).start()
                return 0

            steps = a.shape[1] // EDGE
            lax.fori_loop(0, steps // 2, last, 0)
            copy(steps - 2, 0).wait()
            copy(steps - 1, 1).wait()
        else:
            def last(c, _):
                by[:, at(c, EDGE)] = changed(at(c, EDGE))
                return 0

            lax.fori_loop(0, a.shape[1] // EDGE, last, 0)
            two = pltpu.make_async_copy(by, by_out, osems.at[1])
            two.start()
            two.wait()


def backward(a, h, by, wg, wu, wd, turn_in, turn_out):
    d, tokens = a.shape
    wide, tall = pl.BlockSpec((d, TILE), lambda n: (0, n)), pl.BlockSpec((TILE, d), lambda n: (n, 0))
    return pl.pallas_call(
        functools.partial(backward_kernel, turn_in, turn_out),
        grid=(wg.shape[1] // TILE,),
        in_specs=[ANY, ANY, ANY, wide, wide, tall],
        out_specs=[wide, wide, tall, ANY],
        out_shape=[jax.ShapeDtypeStruct(w.shape, BF16) for w in (wg, wu, wd)] + [jax.ShapeDtypeStruct((tokens, d) if turn_out else (d, tokens), BF16)],
        scratch_shapes=[
            pltpu.VMEM((d, tokens), BF16),
            pltpu.VMEM((d, tokens), BF16),
            pltpu.VMEM((d, tokens), F32),
            pltpu.VMEM((d, TILE), F32),
            pltpu.VMEM((d, TILE), F32),
            pltpu.VMEM((d, TILE), F32),
            pltpu.VMEM((TILE, CHUNK), BF16),
            pltpu.VMEM((TILE, CHUNK), BF16),
            pltpu.VMEM((TILE, CHUNK), BF16),
            pltpu.VMEM((2, EDGE, d), BF16),
            pltpu.SemaphoreType.DMA((2,)),
            pltpu.SemaphoreType.DMA((2,)),
        ],
        compiler_params=pltpu.CompilerParams(vmem_limit_bytes=63 * 2**20, dimension_semantics=("arbitrary",)),
        cost_estimate=pl.CostEstimate(flops=16 * tokens * d * wg.shape[1], bytes_accessed=60 * 2**20, transcendentals=0),
        name="backward_layer",
    )(a, h, by, wg, wu, wd)


def solution(mesh):
    def step(x, dy, *weights):
        def fetched(number):
            return [lax.all_gather(w[number], "s", axis=0, tiled=True) for w in weights]

        def summed(term):
            return lax.psum(lax.psum_scatter(term, "s", scatter_dimension=0, tiled=True), "r")

        first, last = fetched(0), fetched(1)
        xt, a0, h1, a1 = forward(x[0], *first)
        *by_w1, by_h1 = backward(a1, h1, dy[0], *last, turn_in=True, turn_out=False)
        *by_w0, by_x = backward(a0, xt, by_h1, *first, turn_in=False, turn_out=True)
        mine = [[summed(t) for t in by_w0], [summed(t) for t in by_w1]]
        return (by_x[None], *(jnp.stack([mine[0][i], mine[1][i]]) for i in range(3)))

    states, cut = P(("rep", "r", "s"), None, None), P(None, "s", None)
    return jax.shard_map(
        step,
        mesh=mesh,
        in_specs=(states, states) + (cut,) * 3,
        out_specs=(states,) + (P("rep", "s", None),) * 3,
        check_vma=False,
    )
```

time: 864 us -> 1070 us (1.24)
  matrix products: 583 us -> 0 us
  Pallas kernels: 0 us -> 502 us
  waiting for transfers between devices: 178 us -> 539 us
  local copies, waits for them, and re-layouts: 46 us -> 8.02 us
  other arithmetic: 34.9 us -> 5.91 us
    dot_general x17 -> x0, matrix products: 583 us -> none  [the longest x6 224 us: layer(): up = jnp.dot(a, w['w_up'], preferred_element_type=jnp.float32)]
    pallas_call x0 -> x3, Pallas kernels: none -> 502 us  [the longest x2 412 us: backward(): pl.pallas_call(functools.partial(backward_kernel, turn_in, turn_out), gri...]
    reduce_scatter x6, waiting for transfers between devices: 60.6 us -> 254 us  [summed(): lax.psum_scatter(term, 's', scatter_dimension=0, tiled=True)]
    all_gather x6, waiting for transfers between devices: 14.3 us -> 118 us  [fetched(): return [lax.all_gather(w[number], 's', axis=0, tiled=True) for w in weights]]
    psum x1, waiting for transfers between devices: 102 us -> 163 us  [summed(): lax.psum(lax.psum_scatter(term, 's', scatter_dimension=0, tiled=True), 'r')]
    unnamed x23 -> x10, local copies, waits for them, and re-layouts: 36.5 us -> 0.02 us
    broadcast_in_dim x1 -> x0, other arithmetic: 12.4 us -> none  [step(): by_h[None]]
  transfers between devices with their start and end apart: 13 -> 13, of which waited for: 6 -> 11; matrix products, arithmetic and copies ran while one was open for 57% -> 0% of each run, Pallas kernels for 0% -> 8%
where the time goes in v1:
time: 1070 us
  waiting for transfers between devices  539 us (50%)
  Pallas kernels  502 us (47%)
  between operations  14 us (1%)
    pallas_call x2, Pallas kernels, backward(): pl.pallas_call(functools.partial(backward_kernel, turn_in, turn_out), gri...  412 us
    reduce_scatter x6, waiting for transfers between devices, summed(): lax.psum_scatter(term, 's', scatter_dimension=0, tiled=True)  254 us
    psum x1, waiting for transfers between devices, summed(): lax.psum(lax.psum_scatter(term, 's', scatter_dimension=0, tiled=True), 'r')  163 us
    all_gather x6, waiting for transfers between devices, fetched(): return [lax.all_gather(w[number], 's', axis=0, tiled=True) for w in weights]  118 us
    pallas_call x1, Pallas kernels, forward(): pl.pallas_call(forward_kernel, grid=(wg.shape[1] // TILE,), in_specs=[ANY...  90.5 us
  transfers between devices with their start and end apart: 13, of which 11 were waited for; matrix products, arithmetic and copies ran while one was open for 0% of the time, Pallas kernels for 8%

profile of v1, /device:TPU:0, one launch (start us, length us, event | category | flops | bytes accessed | tf_op | source)
XLA Modules:
  0.0 1069.5 jit_solution(15831699420261113237)
XLA Ops:
  7.2 0.0 copy-start
  7.2 0.0 all-gather.13.cloned.1.call-start
  7.2 3.3 fusion.2
  10.5 0.0 all-gather.13.cloned.1.call-update
  10.5 0.0 all-gather.15.cloned.1.call-start
  10.6 1.5 fusion.1
  12.1 0.0 all-gather.15.cloned.1.call-update
  12.1 0.0 all-gather.17.cloned.1.call-start
  12.2 3.2 fusion
  15.4 0.0 all-gather.17.cloned.1.call-update
  15.4 0.0 all-gather.19.cloned.1.call-start
  15.5 0.5 all-gather.19.cloned.1.call-update
  16.0 0.0 all-gather.21.cloned.1.call-start
  16.0 0.5 all-gather.21.cloned.1.call-update
  16.6 0.0 all-gather.23.cloned.1.call-start
  16.6 0.5 all-gather.23.cloned.1.call-update
  17.1 0.0 reduce-scatter.7.cloned.1.call-start
  17.2 30.1 %all-gather.13.cloned.1.call-done = bf16[1,896,2560]{2,1,0:T(8,128)(2,1)} async-done(((bf16[1,224,2560]{2,1,0:T(8,128)(2,1)}), bf16[1,896,2560]{2,1,0:T(8,128)(2,1)}) %all-gather.13.cloned.1.call-update) | async-done | bytes 4587536 | tf_op jit(solution)/shard_map/all_gather | solution.py:241
  47.3 35.9 %all-gather.15.cloned.1.call-done = bf16[1,896,2560]{2,1,0:T(8,128)(2,1)} async-done(((bf16[1,224,2560]{2,1,0:T(8,128)(2,1)}), bf16[1,896,2560]{2,1,0:T(8,128)(2,1)}) %all-gather.15.cloned.1.call-update) | async-done | bytes 4587536 | tf_op jit(solution)/shard_map/all_gather | solution.py:241
  83.2 35.3 %all-gather.17.cloned.1.call-done = bf16[1,2560,896]{2,1,0:T(8,128)(2,1)} async-done(((bf16[1,640,896]{2,1,0:T(8,128)(2,1)}), bf16[1,2560,896]{2,1,0:T(8,128)(2,1)}) %all-gather.17.cloned.1.call-update) | async-done | bytes 4587536 | tf_op jit(solution)/shard_map/all_gather | solution.py:241
  118.5 90.5 %forward_layer.1 = (bf16[896,4096]{1,0:T(8,128)(2,1)}, bf16[896,4096]{1,0:T(8,128)(2,1)}, bf16[896,4096]{1,0:T(8,128)(2,1)}, bf16[896,4096]{1,0:T(8,128)(2,1)}) custom-call(bf16[4096,896]{1,0:T(8,128)(2,1)} %bitcast.21, bf16[896,2560]{1,0:T(8,128)(2,1)} %bitcast.23, bf16[896,2560]{1,0:T(8,128)(2,1)} %bitcast.25, bf16[2560,896]{1,0:T(8,128)(2,1)} %bitcast.27), custom_call_target="tpu_custom_call" | custom-call | flops 56371445760 | bytes 62914560 | tf_op jit(solution)/shard_map/forward_layer/pallas_call | solution.py:101
  209.0 0.0 all-gather.19.cloned.1.call-done
  209.0 0.0 all-gather.21.cloned.1.call-done
  209.1 16.2 %all-gather.23.cloned.1.call-done = bf16[1,2560,896]{2,1,0:T(8,128)(2,1)} async-done(((bf16[1,640,896]{2,1,0:T(8,128)(2,1)}), bf16[1,2560,896]{2,1,0:T(8,128)(2,1)}) %all-gather.23.cloned.1.call-update) | async-done | bytes 4587536 | tf_op jit(solution)/shard_map/all_gather | solution.py:241
  225.2 209.8 %backward_layer.2 = (bf16[896,2560]{1,0:T(8,128)(2,1)}, bf16[896,2560]{1,0:T(8,128)(2,1)}, bf16[2560,896]{1,0:T(8,128)(2,1)}, bf16[896,4096]{1,0:T(8,128)(2,1)}) custom-call(bf16[896,4096]{1,0:T(8,128)(2,1)} %get-tuple-element.18.at_in, bf16[896,4096]{1,0:T(8,128)(2,1)} %get-tuple-element.19.ht_in, bf16[4096,896]{1,0:T(8,128)(2,1)} %bitcast.22, ...), custom_call_target="tpu_custom_call" | custom-call | flops 150323855360 | bytes 62914560 | tf_op jit(solution)/shard_map/backward_layer/pallas_call | solution.py:212
  435.0 201.8 %backward_layer.3 = (bf16[896,2560]{1,0:T(8,128)(2,1)}, bf16[896,2560]{1,0:T(8,128)(2,1)}, bf16[2560,896]{1,0:T(8,128)(2,1)}, bf16[4096,896]{1,0:T(8,128)(2,1)}) custom-call(bf16[896,4096]{1,0:T(8,128)(2,1)} %get-tuple-element.16.at_in, bf16[896,4096]{1,0:T(8,128)(2,1)} %get-tuple-element.17.ht_in, bf16[896,4096]{1,0:T(8,128)(2,1)} %get-tuple-element.20.by_in, ...), custom_call_target="tpu_custom_call" | custom-call | flops 150323855360 | bytes 62914560 | tf_op jit(solution)/shard_map/backward_layer/pallas_call | solution.py:212
  636.8 0.0 reduce-scatter.7.cloned.1.call-update
  636.8 0.0 reduce-scatter.11.cloned.1.call-start
  636.9 0.7 reduce-scatter.11.cloned.1.call-update
  637.6 0.0 reduce-scatter.15.cloned.1.call-start
  637.6 0.7 reduce-scatter.15.cloned.1.call-update
  638.3 0.0 reduce-scatter.9.cloned.1.call-start
  638.4 0.5 reduce-scatter.9.cloned.1.call-update
  638.9 0.0 reduce-scatter.13.cloned.1.call-start
  639.0 0.7 reduce-scatter.13.cloned.1.call-update
  639.7 0.0 reduce-scatter.17.cloned.1.call-start
  639.7 0.5 reduce-scatter.17.cloned.1.call-update
  640.2 0.0 all-reduce.3.cloned.1.call-start
  640.3 37.4 %reduce-scatter.7.cloned.1.call-done = bf16[224,2560]{1,0:T(8,128)(2,1)} async-done(((bf16[896,2560]{1,0:T(8,128)(2,1)}), bf16[224,2560]{1,0:T(8,128)(2,1)}) %reduce-scatter.7.cloned.1.call-update) | async-done | bytes 1146896 | tf_op jit(solution)/shard_map/reduce_scatter | solution.py:244
  677.7 43.3 %reduce-scatter.11.cloned.1.call-done = bf16[224,2560]{1,0:T(8,128)(2,1)} async-done(((bf16[896,2560]{1,0:T(8,128)(2,1)}), bf16[224,2560]{1,0:T(8,128)(2,1)}) %reduce-scatter.11.cloned.1.call-update) | async-done | bytes 1146896 | tf_op jit(solution)/shard_map/reduce_scatter | solution.py:244
  721.0 43.3 %reduce-scatter.15.cloned.1.call-done = bf16[640,896]{1,0:T(8,128)(2,1)} async-done(((bf16[2560,896]{1,0:T(8,128)(2,1)}), bf16[640,896]{1,0:T(8,128)(2,1)}) %reduce-scatter.15.cloned.1.call-update) | async-done | bytes 1146896 | tf_op jit(solution)/shard_map/reduce_scatter | solution.py:244
  764.3 43.1 %reduce-scatter.9.cloned.1.call-done = bf16[224,2560]{1,0:T(8,128)(2,1)} async-done(((bf16[896,2560]{1,0:T(8,128)(2,1)}), bf16[224,2560]{1,0:T(8,128)(2,1)}) %reduce-scatter.9.cloned.1.call-update) | async-done | bytes 1146896 | tf_op jit(solution)/shard_map/reduce_scatter | solution.py:244
  807.4 43.3 %reduce-scatter.13.cloned.1.call-done = bf16[224,2560]{1,0:T(8,128)(2,1)} async-done(((bf16[896,2560]{1,0:T(8,128)(2,1)}), bf16[224,2560]{1,0:T(8,128)(2,1)}) %reduce-scatter.13.cloned.1.call-update) | async-done | bytes 1146896 | tf_op jit(solution)/shard_map/reduce_scatter | solution.py:244
  850.7 43.1 %reduce-scatter.17.cloned.1.call-done = bf16[640,896]{1,0:T(8,128)(2,1)} async-done(((bf16[2560,896]{1,0:T(8,128)(2,1)}), bf16[640,896]{1,0:T(8,128)(2,1)}) %reduce-scatter.17.cloned.1.call-update) | async-done | bytes 1146896 | tf_op jit(solution)/shard_map/reduce_scatter | solution.py:244
  893.9 0.0 all-reduce.3.cloned.1.call-update
  893.9 163.1 %all-reduce.3.cloned.1.call-done = (bf16[1,224,2560]{2,1,0:T(8,128)(2,1)}, bf16[1,224,2560]{2,1,0:T(8,128)(2,1)}, bf16[1,224,2560]{2,1,0:T(8,128)(2,1)}, bf16[1,...) async-done(((bf16[1,224,2560]{2,1,0:T(8,128)(2,1)}, bf16[1,224,2560]{2,1,0:T(8,128)(2,1)}, bf16[1,224,2560]{2,1,0:T(8,128)(2,1)}, ...) | async-done | bytes 6881296 | tf_op jit(solution)/shard_map/psum | solution.py:244
  1057.0 3.4 pad_maximum_fusion.2
  1060.4 2.5 pad_maximum_fusion
  (9 shorter events, 0.0 us)
Async XLA Ops:
  7.2 3.4 copy-start
  7.2 40.1 %all-gather.13.cloned.1.call-start = ((), (), s32[]{:S(2)}) async-start(), calls=%async_computation.12 | async-start | bytes 5734400 | tf_op jit(solution)/shard_map/all_gather | solution.py:241
  10.5 72.7 %all-gather.15.cloned.1.call-start = ((), (), s32[]{:S(2)}) async-start(), calls=%async_computation.13 | async-start | bytes 5734400 | tf_op jit(solution)/shard_map/all_gather | solution.py:241
  12.1 106.4 %all-gather.17.cloned.1.call-start = ((), (), s32[]{:S(2)}) async-start(), calls=%async_computation.14 | async-start | bytes 5734400 | tf_op jit(solution)/shard_map/all_gather | solution.py:241
  15.4 193.6 %all-gather.19.cloned.1.call-start = ((), (), s32[]{:S(2)}) async-start(), calls=%async_computation.15 | async-start | bytes 5734400 | tf_op jit(solution)/shard_map/all_gather | solution.py:241
  16.0 193.1 %all-gather.21.cloned.1.call-start = ((), (), s32[]{:S(2)}) async-start(), calls=%async_computation.16 | async-start | bytes 5734400 | tf_op jit(solution)/shard_map/all_gather | solution.py:241
  16.6 208.7 %all-gather.23.cloned.1.call-start = ((), (), s32[]{:S(2)}) async-start(), calls=%async_computation.17 | async-start | bytes 5734400 | tf_op jit(solution)/shard_map/all_gather | solution.py:241
  17.1 660.6 %reduce-scatter.7.cloned.1.call-start = ((), (), s32[]{:S(2)}) async-start(), calls=%async_computation.6 | async-start | bytes 5734400 | tf_op jit(solution)/shard_map/reduce_scatter | solution.py:244
  636.8 84.2 %reduce-scatter.11.cloned.1.call-start = ((), (), s32[]{:S(2)}) async-start(), calls=%async_computation.8 | async-start | bytes 5734400 | tf_op jit(solution)/shard_map/reduce_scatter | solution.py:244
  637.6 126.7 %reduce-scatter.15.cloned.1.call-start = ((), (), s32[]{:S(2)}) async-start(), calls=%async_computation.10 | async-start | bytes 5734400 | tf_op jit(solution)/shard_map/reduce_scatter | solution.py:244
  638.3 169.1 %reduce-scatter.9.cloned.1.call-start = ((), (), s32[]{:S(2)}) async-start(), calls=%async_computation.7 | async-start | bytes 5734400 | tf_op jit(solution)/shard_map/reduce_scatter | solution.py:244
  638.9 211.8 %reduce-scatter.13.cloned.1.call-start = ((), (), s32[]{:S(2)}) async-start(), calls=%async_computation.9 | async-start | bytes 5734400 | tf_op jit(solution)/shard_map/reduce_scatter | solution.py:244
  639.7 254.2 %reduce-scatter.17.cloned.1.call-start = ((), (), s32[]{:S(2)}) async-start(), calls=%async_computation.11 | async-start | bytes 5734400 | tf_op jit(solution)/shard_map/reduce_scatter | solution.py:244
  640.2 416.8 %all-reduce.3.cloned.1.call-start = ((), (), s32[]{:S(2)}) async-start(), calls=%async_computation.18 | async-start | bytes 13762560 | tf_op jit(solution)/shard_map/psum | solution.py:244
  1057.0 3.4 copy-start.1
  1057.0 3.4 copy-start.2
  1057.0 3.4 copy-start.3
  1057.0 3.4 copy-start.4
Sparse Core Ops, SparseCore 0:
  10.6 36.5 all-gather.12
  49.4 33.7 all-gather.14
  84.7 33.7 all-gather.16
  120.5 33.7 all-gather.18
  156.2 33.7 all-gather.20
  191.4 33.7 all-gather.22
  637.0 40.7 reduce-scatter.6
  680.3 40.7 reduce-scatter.10
  723.5 40.7 reduce-scatter.14
  766.7 40.7 reduce-scatter.8
  810.0 40.7 reduce-scatter.12
  853.1 40.7 reduce-scatter.16
  896.8 160.1 all-reduce.2

commit v2 on v1

--- a/solution.py
+++ b/solution.py
@@ -14,10 +14,21 @@
 SUB = 512
 EDGE = 256
 EPS = 1e-6
+BLOCK = 2688
+HALF = BLOCK // 2
+MESH = pl.DeviceIdType.MESH
 
 
 def dot(a, b, over=(1, 0)):
     return lax.dot_general(a, b, (((over[0],), (over[1],)), ((), ())), preferred_element_type=F32)
+
+
+def flat(w):
+    return w[...].reshape(-1, w.shape[-1])
+
+
+def tiles_of(w):
+    return pl.BlockSpec((w.shape[0], None, *w.shape[2:]), lambda n: (0, n, 0, 0))
 
 
 def at(step, size):
@@ -69,9 +80,9 @@
     def step(c, _):
         for i in range(CHUNK // SUB):
             tokens = pl.ds(pl.multiple_of(c * CHUNK + i * SUB, SUB), SUB)
-            g, u = dot(wg[...], a[:, tokens], (0, 0)), dot(wu[...], a[:, tokens], (0, 0))
+            g, u = dot(flat(wg), a[:, tokens], (0, 0)), dot(flat(wu), a[:, tokens], (0, 0))
             p[:, pl.ds(i * SUB, SUB)] = (g * jax.nn.sigmoid(g) * u).astype(BF16)
-        total[:, at(c, CHUNK)] += dot(wd[...], p[...], (0, 0))
+        total[:, at(c, CHUNK)] += dot(flat(wd), p[...], (0, 0))
         return 0
 
     lax.fori_loop(0, chunks, step, 0)
@@ -100,8 +111,8 @@
     state = jax.ShapeDtypeStruct((d, tokens), BF16)
     return pl.pallas_call(
         forward_kernel,
-        grid=(wg.shape[1] // TILE,),
-        in_specs=[ANY, pl.BlockSpec((d, TILE), lambda n: (0, n)), pl.BlockSpec((d, TILE), lambda n: (0, n)), pl.BlockSpec((TILE, d), lambda n: (n, 0))],
+        grid=(wg.shape[1],),
+        in_specs=[ANY, *map(tiles_of, (wg, wu, wd))],
         out_specs=[ANY] * 4,
         out_shape=[state] * 4,
         scratch_shapes=[
@@ -114,28 +125,130 @@
             pltpu.SemaphoreType.DMA((2,)),
         ],
         compiler_params=pltpu.CompilerParams(vmem_limit_bytes=63 * 2**20, dimension_semantics=("arbitrary",)),
-        cost_estimate=pl.CostEstimate(flops=6 * tokens * d * wg.shape[1], bytes_accessed=60 * 2**20, transcendentals=0),
+        cost_estimate=pl.CostEstimate(flops=6 * tokens * d * TILE * wg.shape[1], bytes_accessed=60 * 2**20, transcendentals=0),
         name="forward_layer",
     )(x, wg, wu, wd)
 
 
-def backward_kernel(turn_in, turn_out, at_in, ht_in, by_in, wg, wu, wd, og, ou, od, by_out, a, by, total, accg, accu, accd, p, dg, du, stage, sems, osems):
+def backward_kernel(final, *refs):
+    refs = iter(refs)
+    take = lambda count: [next(refs) for _ in range(count)]
+    at_in, ht_in, by_in, wg, wu, wd = take(6)
+    if final:
+        kept_in, sent_in = take(2)
+        by_out, sums_out = take(2)
+    else:
+        by_out, sums_out, kept_out, sent_out = take(4)
+    a, by, total, accg, accu, accd, p, dg, du, stage = take(10)
+    kept, send_d, recv_d, send_x, recv_x, send_y, recv_y, done = take(8)
+    sems, osems, ssem, rsem, free = take(5)
+
     n, passes = pl.program_id(0), pl.num_programs(0)
-    chunks = a.shape[1] // CHUNK
+    chunks, steps = a.shape[1] // CHUNK, a.shape[1] // EDGE
+    s, r = lax.axis_index("s"), lax.axis_index("r")
+    x, core = s // 2, s % 2
+    partner, across, beside = {"s": s + 1 - 2 * core}, {"s": (s + 2) % 4}, {"r": 1 - r}
+    jobs = 6 if final else 4
+    mine, other = pl.ds(pl.multiple_of(r * HALF, HALF), HALF), pl.ds(pl.multiple_of((1 - r) * HALF, HALF), HALF)
+
+    def remote(number, source, target, device):
+        return pltpu.make_async_remote_copy(source, target, ssem.at[number], rsem.at[number], device_id=device, device_id_type=MESH)
+
+    to_partner = remote(0, send_d, recv_d, partner)
+    to_across = remote(1, send_x, recv_x, across)
+    to_beside = remote(2, send_y, recv_y, beside)
+    back_beside = remote(3, done.at[mine, :], done.at[mine, :], beside)
+    devices = (partner, across, beside, beside)
+
+    def send(number, copy, job):
+        @pl.when(job > 0)
+        def _():
+            pl.semaphore_wait(free.at[number], 1)
+
+        copy.start()
+
+    def freed(number, job):
+        @pl.when(job < jobs - 1)
+        def _():
+            pl.semaphore_signal(free.at[number], 1, device_id=devices[number], device_id_type=MESH)
+
+    def cut(owner, write):
+        rows = pl.ds(pl.multiple_of(owner * 224, 32), 224)
+        for k in range(4):
+            write(k * 224, 224, accg[rows, k * 128 : k * 128 + 128])
+            write(896 + k * 224, 224, accu[rows, k * 128 : k * 128 + 128])
+        write(1792, 896, accd[:, pl.ds(pl.multiple_of(owner * 128, 128), 128)])
+
+    def pack():
+        for slot, place in ((0, x), (1, 1 - x)):
+            def keep(first, size, value, slot=slot):
+                kept[slot, first : first + size, :] = value
+
+            def leave(first, size, value, slot=slot):
+                send_d[slot, first : first + size, :] = value.astype(BF16)
+
+            cut(2 * place + core, keep)
+            cut(2 * place + 1 - core, leave)
+
+    def after_partner(job):
+        to_partner.wait_recv()
+        to_partner.wait_send()
+        send_x[...] = (kept[1] + recv_d[1].astype(F32)).astype(BF16)
+        kept[0] = kept[0] + recv_d[0].astype(F32)
+        freed(0, job)
+        send(1, to_across, job)
+
+    def after_across(job):
+        to_across.wait_recv()
+        to_across.wait_send()
+        kept[0] = kept[0] + recv_x[...].astype(F32)
+        send_y[...] = kept[0, other, :].astype(BF16)
+        freed(1, job)
+        send(2, to_beside, job)
+
+    def after_beside(job):
+        to_beside.wait_recv()
+        to_beside.wait_send()
+        done[mine, :] = (kept[0, mine, :] + recv_y[...].astype(F32)).astype(BF16)
+        freed(2, job)
+        send(3, back_beside, job)
+
+    def written(job):
+        return pltpu.make_async_copy(done, sums_out.at[job], osems.at[2])
+
+    def whole(job):
+        back_beside.wait_recv()
+        back_beside.wait_send()
+        written(job).start()
+
+    def written_out(job):
+        written(job).wait()
+        freed(3, job)
+
+    job = n if final else n - 1
 
     @pl.when(n == 0)
     def _():
+        barrier = pltpu.get_barrier_semaphore()
+        for device in (partner, across, beside):
+            pl.semaphore_signal(barrier, 1, device_id=device, device_id_type=MESH)
         one = pltpu.make_async_copy(at_in, a, osems.at[0])
         one.start()
-        if turn_in:
+        if final:
+            two = pltpu.make_async_copy(by_in, by, osems.at[1])
+            two.start()
+            three, four = pltpu.make_async_copy(kept_in, kept, sems.at[0]), pltpu.make_async_copy(sent_in, send_d, sems.at[1])
+            three.start(), four.start()
+            three.wait(), four.wait()
+        pl.semaphore_wait(barrier, 3)
+        if final:
+            send(0, to_partner, job)
+            two.wait()
+        else:
             def write(c, t):
                 by[:, at(c, EDGE)] = t
 
             turned(by_in, stage, sems, write)
-        else:
-            two = pltpu.make_async_copy(by_in, by, osems.at[1])
-            two.start()
-            two.wait()
         total[...] = jnp.zeros_like(total)
         one.wait()
 
@@ -145,30 +258,64 @@
 
     def step(c, _):
         cols = at(c, CHUNK)
+        gate, up, down = flat(wg), flat(wu), flat(wd)
         for i in range(CHUNK // SUB):
             tokens, q = pl.ds(pl.multiple_of(c * CHUNK + i * SUB, SUB), SUB), pl.ds(i * SUB, SUB)
-            g, u = dot(wg[...], a[:, tokens], (0, 0)), dot(wu[...], a[:, tokens], (0, 0))
-            dp = dot(wd[...], by[:, tokens]).astype(BF16).astype(F32)
+            g, u = dot(gate, a[:, tokens], (0, 0)), dot(up, a[:, tokens], (0, 0))
+            dp = dot(down, by[:, tokens]).astype(BF16).astype(F32)
             sg = jax.nn.sigmoid(g)
-            s = g * sg
-            p[:, q] = (s * u).astype(BF16)
-            du[:, q] = (dp * s).astype(BF16)
-            dg[:, q] = (dp * u * (sg + s * (1 - sg))).astype(BF16)
-        total[:, cols] += dot(wg[...], dg[...]) + dot(wu[...], du[...])
+            t = g * sg
+            p[:, q] = (t * u).astype(BF16)
+            du[:, q] = (dp * t).astype(BF16)
+            dg[:, q] = (dp * u * (sg + t * (1 - sg))).astype(BF16)
+        total[:, cols] += dot(gate, dg[...]) + dot(up, du[...])
         accg[...] += dot(a[:, cols], dg[...], (1, 1))
         accu[...] += dot(a[:, cols], du[...], (1, 1))
         accd[...] += dot(by[:, cols], p[...], (1, 1))
+
+        @pl.when((c == 0) & (job >= 0))
+        def _():
+            after_partner(job)
+
+        @pl.when((c == 0) & (job >= 1))
+        def _():
+            whole(job - 1)
+
+        @pl.when((c == 1) & (job >= 1))
+        def _():
+            written_out(job - 1)
+
+        @pl.when((c == 2) & (job >= 0))
+        def _():
+            after_across(job)
+
         return 0
 
     lax.fori_loop(0, chunks, step, 0)
-    og[...] = accg[...].astype(BF16)
-    ou[...] = accu[...].astype(BF16)
-    od[...] = accd[...].T.astype(BF16)
+
+    @pl.when(job >= 0)
+    def _():
+        after_beside(job)
+
+    pack()
+
+    if final:
+        send(0, to_partner, job + 1)
+    else:
+        @pl.when(n < passes - 1)
+        def _():
+            send(0, to_partner, job + 1)
 
     @pl.when(n == passes - 1)
     def _():
         one = pltpu.make_async_copy(ht_in, a, osems.at[0])
         one.start()
+        if final:
+            whole(4)
+            after_partner(5)
+        else:
+            three, four = pltpu.make_async_copy(kept, kept_out, sems.at[0]), pltpu.make_async_copy(send_d, sent_out, sems.at[1])
+            three.start(), four.start()
         one.wait()
 
         def changed(cols):
@@ -177,7 +324,7 @@
             dh = (f * da - h * (f * f * f * jnp.mean(da * h, 0, keepdims=True))).astype(BF16)
             return (by[:, cols].astype(F32) + dh.astype(F32)).astype(BF16)
 
-        if turn_out:
+        if final:
             def copy(c, slot):
                 return pltpu.make_async_copy(stage.at[slot], by_out.at[at(c, EDGE), :], sems.at[slot])
 
@@ -191,30 +338,40 @@
                     copy(2 * c + slot, slot).start()
                 return 0
 
-            steps = a.shape[1] // EDGE
             lax.fori_loop(0, steps // 2, last, 0)
             copy(steps - 2, 0).wait()
             copy(steps - 1, 1).wait()
+            written_out(4)
+            after_across(5)
+            after_beside(5)
+            whole(5)
+            written_out(5)
         else:
             def last(c, _):
                 by[:, at(c, EDGE)] = changed(at(c, EDGE))
                 return 0
 
-            lax.fori_loop(0, a.shape[1] // EDGE, last, 0)
+            lax.fori_loop(0, steps, last, 0)
             two = pltpu.make_async_copy(by, by_out, osems.at[1])
             two.start()
+            whole(3)
+            written_out(3)
+            three.wait(), four.wait()
             two.wait()
 
 
-def backward(a, h, by, wg, wu, wd, turn_in, turn_out):
+def backward(a, h, by, wg, wu, wd, waiting=None):
     d, tokens = a.shape
-    wide, tall = pl.BlockSpec((d, TILE), lambda n: (0, n)), pl.BlockSpec((TILE, d), lambda n: (n, 0))
+    final = waiting is not None
+    sums = lambda count: jax.ShapeDtypeStruct((count, BLOCK, 128), BF16)
+    state = jax.ShapeDtypeStruct((tokens, d) if final else (d, tokens), BF16)
+    handed = [] if final else [jax.ShapeDtypeStruct((2, BLOCK, 128), F32), sums(2)]
     return pl.pallas_call(
-        functools.partial(backward_kernel, turn_in, turn_out),
-        grid=(wg.shape[1] // TILE,),
-        in_specs=[ANY, ANY, ANY, wide, wide, tall],
-        out_specs=[wide, wide, tall, ANY],
-        out_shape=[jax.ShapeDtypeStruct(w.shape, BF16) for w in (wg, wu, wd)] + [jax.ShapeDtypeStruct((tokens, d) if turn_out else (d, tokens), BF16)],
+        functools.partial(backward_kernel, final),
+        grid=(wg.shape[1],),
+        in_specs=[ANY, ANY, ANY, *map(tiles_of, (wg, wu, wd))] + [ANY, ANY] * final,
+        out_specs=[ANY] * (2 + len(handed)),
+        out_shape=[state, sums(6 if final else 4), *handed],
         scratch_shapes=[
             pltpu.VMEM((d, tokens), BF16),
             pltpu.VMEM((d, tokens), BF16),
@@ -226,29 +383,47 @@
             pltpu.VMEM((TILE, CHUNK), BF16),
             pltpu.VMEM((TILE, CHUNK), BF16),
             pltpu.VMEM((2, EDGE, d), BF16),
+            pltpu.VMEM((2, BLOCK, 128), F32),
+            pltpu.VMEM((2, BLOCK, 128), BF16),
+            pltpu.VMEM((2, BLOCK, 128), BF16),
+            pltpu.VMEM((BLOCK, 128), BF16),
+            pltpu.VMEM((BLOCK, 128), BF16),
+            pltpu.VMEM((HALF, 128), BF16),
+            pltpu.VMEM((HALF, 128), BF16),
+            pltpu.VMEM((BLOCK, 128), BF16),
             pltpu.SemaphoreType.DMA((2,)),
-            pltpu.SemaphoreType.DMA((2,)),
+            pltpu.SemaphoreType.DMA((3,)),
+            pltpu.SemaphoreType.DMA((4,)),
+            pltpu.SemaphoreType.DMA((4,)),
+            pltpu.SemaphoreType.REGULAR((4,)),
         ],
-        compiler_params=pltpu.CompilerParams(vmem_limit_bytes=63 * 2**20, dimension_semantics=("arbitrary",)),
-        cost_estimate=pl.CostEstimate(flops=16 * tokens * d * wg.shape[1], bytes_accessed=60 * 2**20, transcendentals=0),
-        name="backward_layer",
-    )(a, h, by, wg, wu, wd)
+        compiler_params=pltpu.CompilerParams(
+            vmem_limit_bytes=63 * 2**20, dimension_semantics=("arbitrary",), collective_id=1 + final, has_side_effects=True
+        ),
+        cost_estimate=pl.CostEstimate(flops=16 * tokens * d * TILE * wg.shape[1], bytes_accessed=60 * 2**20, transcendentals=0),
+        name="backward_final" if final else "backward_layer",
+    )(a, h, by, wg, wu, wd, *(waiting or ()))
 
 
 def solution(mesh):
     def step(x, dy, *weights):
+        def cut(w):
+            return w.reshape(w.shape[0], 4, 5, 128).transpose(2, 0, 1, 3).reshape(5, w.shape[0], 512)
+
         def fetched(number):
-            return [lax.all_gather(w[number], "s", axis=0, tiled=True) for w in weights]
-
-        def summed(term):
-            return lax.psum(lax.psum_scatter(term, "s", scatter_dimension=0, tiled=True), "r")
+            gate, up, down = (w[number] for w in weights)
+            return [lax.all_gather(w, "s") for w in (cut(gate), cut(up), down.reshape(5, 128, down.shape[1]))]
+
+        def joined(tiles):
+            wide = lambda t: t.reshape(5, 4, 224, 128).transpose(2, 1, 0, 3).reshape(224, 2560)
+            return wide(tiles[:, :896]), wide(tiles[:, 896:1792]), tiles[:, 1792:].transpose(0, 2, 1).reshape(640, 896)
 
         first, last = fetched(0), fetched(1)
         xt, a0, h1, a1 = forward(x[0], *first)
-        *by_w1, by_h1 = backward(a1, h1, dy[0], *last, turn_in=True, turn_out=False)
-        *by_w0, by_x = backward(a0, xt, by_h1, *first, turn_in=False, turn_out=True)
-        mine = [[summed(t) for t in by_w0], [summed(t) for t in by_w1]]
-        return (by_x[None], *(jnp.stack([mine[0][i], mine[1][i]]) for i in range(3)))
+        by_h1, early, *waiting = backward(a1, h1, dy[0], *last)
+        by_x, late = backward(a0, xt, by_h1, *first, waiting)
+        layers = joined(late[1:]), joined(jnp.concatenate([early, late[:1]]))
+        return (by_x[None], *(jnp.stack([layer[i] for layer in layers]) for i in range(3)))
 
     states, cut = P(("rep", "r", "s"), None, None), P(None, "s", None)
     return jax.shard_map(

time: 1070 us -> 725 us (0.68)
  waiting for transfers between devices: 539 us -> 102 us
  local copies, waits for them, and re-layouts: 8.02 us -> 59.6 us
  Pallas kernels: 502 us -> 537 us
    reduce_scatter x6 -> x0, waiting for transfers between devices: 254 us -> none  [summed(): lax.psum_scatter(term, 's', scatter_dimension=0, tiled=True)]
    psum x1 -> x0, waiting for transfers between devices: 163 us -> none  [summed(): lax.psum(lax.psum_scatter(term, 's', scatter_dimension=0, tiled=True), 'r')]
    pallas_call x3, Pallas kernels: 502 us -> 537 us  [the longest x2 447 us: backward(): pl.pallas_call(functools.partial(backward_kernel, final), grid=(wg.shape[...]
    all_gather x6, waiting for transfers between devices: 118 us -> 101 us  [fetched(): lax.all_gather(w, 's')]
    transpose x0 -> x7, local copies, waits for them, and re-layouts: none -> 15 us  [the longest x4 7.75 us: cut(): w.reshape(w.shape[0], 4, 5, 128).transpose(2, 0, 1, 3)]
    unnamed x10 -> x5, local copies, waits for them, and re-layouts: 0.02 us -> 11.7 us
    another operation x0 -> x4, local copies, waits for them, and re-layouts: none -> 10.9 us  [fetched(): lax.all_gather(w, 's')]
  transfers between devices with their start and end apart: 13 -> 6, of which waited for: 11 -> 4; matrix products, arithmetic and copies ran while one was open for 0% -> 3% of each run, Pallas kernels for 8% -> 12%
where the time goes in v2:
time: 725 us; the launch traced here: 724 us
  Pallas kernels  537 us (74%)
  waiting for transfers between devices  102 us (14%)
  local copies, waits for them, and re-layouts  59.6 us (8%)
  between operations  14.2 us (2%)
  other arithmetic  11 us (2%)
    pallas_call x2, Pallas kernels, backward(): pl.pallas_call(functools.partial(backward_kernel, final), grid=(wg.shape[...  447 us
    all_gather x6, waiting for transfers between devices, fetched(): lax.all_gather(w, 's')  101 us
    pallas_call x1, Pallas kernels, forward(): pl.pallas_call(forward_kernel, grid=(wg.shape[1],), in_specs=[ANY, *map(t...  90.3 us
  transfers between devices with their start and end apart: 6, of which 4 were waited for; matrix products, arithmetic and copies ran while one was open for 3% of the time, Pallas kernels for 12%

profile of v2, /device:TPU:0, one launch (start us, length us, event | category | flops | bytes accessed | tf_op | source)
XLA Modules:
  0.0 723.8 jit_solution(8234908495048608544)
XLA Ops:
  7.2 0.0 all-gather.7.cloned.1.call-start
  7.2 2.8 fusion.5
  10.0 1.6 copy.45
  11.5 2.1 copy.46
  13.6 3.2 all_gather_reshape.12
  16.8 0.0 all-gather.7.cloned.1.call-update
  16.8 0.0 all-gather.9.cloned.1.call-start
  16.8 3.1 fusion.4
  20.0 1.6 copy.47
  21.5 2.1 copy.48
  23.6 3.2 all_gather_reshape.13
  26.8 0.0 all-gather.9.cloned.1.call-update
  26.8 0.0 all-gather.11.cloned.1.call-start
  26.8 3.2 fusion.3
  30.0 0.0 all-gather.13.cloned.1.call-start
  30.1 0.6 copy.49
  30.7 2.1 copy.50
  32.8 3.3 all_gather_reshape.14
  36.1 0.0 all-gather.15.cloned.1.call-start
  36.1 0.6 copy.51
  36.7 1.6 copy.52
  38.3 1.3 all_gather_reshape.15
  39.6 0.0 all-gather.17.cloned.1.call-start
  39.6 0.5 all-gather.17.cloned.1.call-update
  40.2 13.4 %all-gather.7.cloned.1.call-done.wg.refs_3_ = bf16[4,5,224,512]{3,2,1,0:T(8,128)(2,1)} async-done(((bf16[1,5,224,512]{3,2,1,0:T(8,128)(2,1)}), bf16[4,5,224,512]{3,2,1,0:T(8,128)(2,1)}) %all-gather.7.cloned.1.call-update) | async-done | bytes 4587536 | tf_op jit(solution)/shard_map/all_gather | solution.py:415
  53.5 35.9 %all-gather.9.cloned.1.call-done.wu.refs_4_ = bf16[4,5,224,512]{3,2,1,0:T(8,128)(2,1)} async-done(((bf16[1,5,224,512]{3,2,1,0:T(8,128)(2,1)}), bf16[4,5,224,512]{3,2,1,0:T(8,128)(2,1)}) %all-gather.9.cloned.1.call-update) | async-done | bytes 4587536 | tf_op jit(solution)/shard_map/all_gather | solution.py:415
  89.5 35.3 %all-gather.11.cloned.1.call-done.wd.refs_5_ = bf16[4,5,128,896]{3,2,1,0:T(8,128)(2,1)} async-done(((bf16[1,5,128,896]{3,2,1,0:T(8,128)(2,1)}), bf16[4,5,128,896]{3,2,1,0:T(8,128)(2,1)}) %all-gather.11.cloned.1.call-update) | async-done | bytes 4587536 | tf_op jit(solution)/shard_map/all_gather | solution.py:415
  124.8 90.3 %forward_layer.1 = (bf16[896,4096]{1,0:T(8,128)(2,1)}, bf16[896,4096]{1,0:T(8,128)(2,1)}, bf16[896,4096]{1,0:T(8,128)(2,1)}, bf16[896,4096]{1,0:T(8,128)(2,1)}) custom-call(bf16[4096,896]{1,0:T(8,128)(2,1)} %bitcast.56, bf16[4,5,224,512]{3,2,1,0:T(8,128)(2,1)} %all-gather.7.cloned.1.call-done.wg.refs_3_, ...), custom_call_target="tpu_custom_call" | custom-call | flops 56371445760 | bytes 62914560 | tf_op jit(solution)/shard_map/forward_layer/pallas_call | solution.py:112
  215.1 0.0 all-gather.13.cloned.1.call-done.refs_3_
  215.1 0.0 all-gather.15.cloned.1.call-done.refs_4_
  215.1 16.4 %all-gather.17.cloned.1.call-done.refs_5_ = bf16[4,5,128,896]{3,2,1,0:T(8,128)(2,1)} async-done(((bf16[1,5,128,896]{3,2,1,0:T(8,128)(2,1)}), bf16[4,5,128,896]{3,2,1,0:T(8,128)(2,1)}) %all-gather.17.cloned.1.call-update) | async-done | bytes 4587536 | tf_op jit(solution)/shard_map/all_gather | solution.py:415
  231.5 215.3 %backward_layer.1 = (bf16[896,4096]{1,0:T(8,128)(2,1)}, bf16[4,2688,128]{2,1,0:T(8,128)(2,1)}, f32[2,2688,128]{2,1,0:T(8,128)}, bf16[2,2688,128]{2,1,0:T(8,128)(2,1)}) custom-call(bf16[896,4096]{1,0:T(8,128)(2,1)} %get-tuple-element.16.refs_0_, bf16[896,4096]{1,0:T(8,128)(2,1)} %get-tuple-element.17.refs_1_, bf16[4096,896]{1,0:T(8,128)(2,1)} %bitcast.57, ...), custom_call_target="tpu_custom_call" | custom-call | flops 150323855360 | bytes 62914560 | tf_op jit(solution)/shard_map/backward_layer/pallas_call | solution.py:369
  446.8 231.6 %backward_final.1 = (bf16[4096,896]{1,0:T(8,128)(2,1)}, bf16[6,2688,128]{2,1,0:T(8,128)(2,1)}) custom-call(bf16[896,4096]{1,0:T(8,128)(2,1)} %get-tuple-element.14.refs_0_, bf16[896,4096]{1,0:T(8,128)(2,1)} %get-tuple-element.15.refs_1_, bf16[896,4096]{1,0:T(8,128)(2,1)} %get-tuple-element.18.refs_2_, ...), custom_call_target="tpu_custom_call" | custom-call | flops 150323855360 | bytes 62914560 | tf_op jit(solution)/shard_map/backward_final/pallas_call | solution.py:369
  678.4 2.0 slice.50
  680.3 3.2 slice_bitcast_fusion
  683.5 1.6 copy.57
  685.2 3.3 fusion.2
  688.5 2.4 copy.58
  690.9 1.4 copy.54
  692.3 1.4 copy.55
  693.7 1.4 copy.56
  695.2 2.2 pad_maximum_fusion.1
  697.4 2.5 copy.60
  699.9 2.4 copy.53
  702.3 2.2 pad_maximum_fusion
  704.5 2.5 copy.59
  707.0 3.2 pad_maximum_fusion.2
  710.2 6.7 copy.62
  (5 shorter events, 0.1 us)
Async XLA Ops:
  7.2 46.4 %all-gather.7.cloned.1.call-start = ((), (), s32[]{:S(2)}) async-start(), calls=%async_computation | async-start | bytes 5734400 | tf_op jit(solution)/shard_map/all_gather | solution.py:415
  16.8 72.7 %all-gather.9.cloned.1.call-start = ((), (), s32[]{:S(2)}) async-start(), calls=%async_computation.1 | async-start | bytes 5734400 | tf_op jit(solution)/shard_map/all_gather | solution.py:415
  26.8 98.0 %all-gather.11.cloned.1.call-start = ((), (), s32[]{:S(2)}) async-start(), calls=%async_computation.2 | async-start | bytes 5734400 | tf_op jit(solution)/shard_map/all_gather | solution.py:415
  30.0 185.1 %all-gather.13.cloned.1.call-start = ((), (), s32[]{:S(2)}) async-start(), calls=%async_computation.3 | async-start | bytes 5734400 | tf_op jit(solution)/shard_map/all_gather | solution.py:415
  32.8 3.3 copy-start
  36.1 179.1 %all-gather.15.cloned.1.call-start = ((), (), s32[]{:S(2)}) async-start(), calls=%async_computation.4 | async-start | bytes 5734400 | tf_op jit(solution)/shard_map/all_gather | solution.py:415
  39.6 191.9 %all-gather.17.cloned.1.call-start = ((), (), s32[]{:S(2)}) async-start(), calls=%async_computation.5 | async-start | bytes 5734400 | tf_op jit(solution)/shard_map/all_gather | solution.py:415
Sparse Core Ops, SparseCore 0:
  16.9 36.5 all-gather.6
  55.6 33.7 all-gather.8
  91.0 33.7 all-gather.10
  126.2 33.7 all-gather.12
  161.9 33.7 all-gather.14
  197.7 33.7 all-gather.16

commit v3 on v1

v3 whole, which is shorter than its diff:
```python
import functools

import jax
import jax.numpy as jnp
from jax import lax
from jax.experimental import pallas as pl
from jax.experimental.pallas import tpu as pltpu
from jax.sharding import PartitionSpec as P

F32, BF16 = jnp.float32, jnp.bfloat16
ANY = pl.BlockSpec(memory_space=pl.ANY)
TILE = 512
CHUNK = 1024
SUB = 512
EDGE = 256
EPS = 1e-6
TN, NT = (0, 0), (1, 1)
PAIR = pltpu.SemaphoreType.DMA((2,))
BLOCK = 2688
HALF = BLOCK // 2
MESH = pl.DeviceIdType.MESH
GATHER = 1, 3, 6, 8, 10, 12, 15, 17


def dot(a, b, over=(1, 0)):
    return lax.dot_general(a, b, (((over[0],), (over[1],)), ((), ())), preferred_element_type=F32)


def at(step, size):
    return pl.ds(pl.multiple_of(step * size, size), size)


def scale_of(h):
    return lax.rsqrt(jnp.mean(h * h, 0, keepdims=True) + EPS)


def turned(source, stage, sems, write):
    chunks = source.shape[0] // EDGE

    def copy(c, slot):
        return pltpu.make_async_copy(source.at[at(c, EDGE), :], stage.at[slot], sems.at[slot])

    copy(0, 0).start()
    copy(1, 1).start()

    def step(c, _):
        for slot in range(2):
            copy(2 * c + slot, slot).wait()
            write(2 * c + slot, stage[slot].T, slot)

            @pl.when(2 * c + slot + 2 < chunks)
            def _():
                copy(2 * c + slot + 2, slot).start()
        return 0

    lax.fori_loop(0, chunks // 2, step, 0)


def forward_kernel(x, gate, up, down, xt_out, at_out, ht_out, at1_out, wg_out, wu_out, wd_out, gu_out, *refs):
    wg, wu, wd, a, total, p, stage, turn, both, sems, osems, own, done, ssem, rsem, tsem, bsem = refs
    n, passes = pl.program_id(0), pl.num_programs(0)
    chunks, tiles = a.shape[1] // CHUNK, wg.shape[0]
    s, r = lax.axis_index("s"), lax.axis_index("r")
    core = s % 2
    partner, across, beside = {"s": s + 1 - 2 * core}, {"s": (s + 2) % 4}, {"r": 1 - r}
    there = (s + 2) % 4

    def rows(ref, size, owner, half=None):
        if half is None:
            return pl.ds(pl.multiple_of(owner * size, size), size)
        return pl.ds(pl.multiple_of(owner * size + half * (size // 2), 16), size // 2)

    def sent(flow, j, device, owner, half=None):
        for ref, size in ((wg, 224), (wu, 224), (wd, 128)):
            part = ref.at[j, rows(ref, size, owner, half), :]
            pltpu.make_async_remote_copy(part, part, ssem.at[flow, j], rsem.at[flow, j], device_id=device, device_id_type=MESH).start()

    def came(sem, j, half=False):
        part = wg.at[j, pl.ds(0, 336 if half else 672), :]
        pltpu.make_async_copy(part, part, sem).wait()

    def load(j, _):
        layer, tile = j // passes, j % passes
        for k in range(4):
            columns = pl.ds(pl.multiple_of(640 * k + 128 * tile, 128), 128)
            for source, ref in ((gate, wg), (up, wu)):
                pltpu.make_async_copy(source.at[layer, :, columns], ref.at[j, rows(ref, 224, s), pl.ds(128 * k, 128)], own.at[j]).start()
        pltpu.make_async_copy(down.at[layer, pl.ds(pl.multiple_of(128 * tile, 128), 128), :], wd.at[j, rows(wd, 128, s), :], own.at[j]).start()
        return 0

    def leave(j, _):
        came(own.at[j], j)
        sent(1, j, across, s, r)
        sent(0, j, partner, s)
        return 0

    def stores(j):
        return [pltpu.make_async_copy(ref.at[j], out.at[j], done.at[i, j]) for i, (ref, out) in enumerate(((wg, wg_out), (wu, wu_out), (wd, wd_out)))]

    def complete(j):
        came(rsem.at[0, j], j)
        came(rsem.at[3, j], j)
        for copy in stores(j):
            copy.start()

    def crossed(j):
        came(rsem.at[1, j], j, True)
        sent(2, j, beside, there, r)

    def joined(j):
        came(rsem.at[2, j], j, True)
        sent(3, j, partner, there)

    def kept_x(c, slot):
        return pltpu.make_async_copy(turn.at[slot], xt_out.at[:, at(c, EDGE)], tsem.at[slot])

    def kept_both(c, i):
        tokens = pl.ds(pl.multiple_of(c * CHUNK + i * SUB, SUB), SUB)
        return pltpu.make_async_copy(both.at[c % 2, i], gu_out.at[:, at(n, TILE), tokens], bsem.at[c % 2, i])

    @pl.when(n == 0)
    def _():
        barrier = pltpu.get_barrier_semaphore()
        for device in (partner, across, beside):
            pl.semaphore_signal(barrier, 1, device_id=device, device_id_type=MESH)
        lax.fori_loop(0, tiles, load, 0)
        pl.semaphore_wait(barrier, 3)
        lax.fori_loop(0, tiles, leave, 0)

        def write(c, ht, slot):
            h = ht.astype(F32)

            @pl.when(c >= 2)
            def _():
                kept_x(c - 2, slot).wait()

            turn[slot] = ht
            kept_x(c, slot).start()
            a[:, at(c, EDGE)] = (h * scale_of(h)).astype(BF16)

        turned(x, stage, sems, write)
        for slot in range(2):
            kept_x(a.shape[1] // EDGE - 2 + slot, slot).wait()
        pltpu.make_async_copy(a, at_out, osems.at[1]).start()
        total[:] = jnp.zeros_like(total)
        crossed(0)
        joined(0)
        crossed(1)
        complete(0)

    def further(j):
        if j > 2:
            complete(j - 2)
        if j - 1 < tiles:
            joined(j - 1)
        if j < tiles:
            crossed(j)

    def step(c, _):
        q = n * chunks + c

        @pl.when(q > 1)
        def _():
            for i in range(CHUNK // SUB):
                kept_both(c, i).wait()

        for i in range(CHUNK // SUB):
            tokens = pl.ds(pl.multiple_of(c * CHUNK + i * SUB, SUB), SUB)
            g, u = dot(wg[n], a[:, tokens], TN), dot(wu[n], a[:, tokens], TN)
            both[c % 2, i, 0], both[c % 2, i, 1] = g, u
            p[:, pl.ds(i * SUB, SUB)] = (g * jax.nn.sigmoid(g) * u).astype(BF16)
        total[:, at(c, CHUNK)] += dot(wd[n], p[:], TN)
        for i in range(CHUNK // SUB):
            kept_both(c, i).start()
        for j, when in enumerate(GATHER, 2):
            pl.when(q == when)(functools.partial(further, j))

        return 0

    lax.fori_loop(0, chunks, step, 0)

    @pl.when(n == passes - 1)
    def _():
        pltpu.make_async_copy(a, at_out, osems.at[1]).wait()
        for c in (chunks - 2, chunks - 1):
            for i in range(CHUNK // SUB):
                kept_both(c, i).wait()

        def ended(j, _):
            for copy in stores(j):
                copy.wait()
            for flow in range(4):
                came(ssem.at[flow, j], j, flow in (1, 2))
            return 0

        parts = a.shape[1] // TILE
        lax.fori_loop(0, parts, ended, 0)

        def move(k, back):
            out = (ht_out if back else xt_out).at[:, at(k, TILE)]
            return pltpu.make_async_copy(*((wg.at[k], out) if back else (out, wg.at[k])), own.at[k])

        for k in range(parts):
            move(k, False).start()

        def last(k, _):
            cols = at(k, TILE)
            move(k, False).wait()
            h = (wg[k].astype(F32) + total[:, cols].astype(BF16).astype(F32)).astype(BF16)
            wg[k] = h
            move(k, True).start()
            h = h.astype(F32)
            a[:, cols] = (h * scale_of(h)).astype(BF16)
            return 0

        lax.fori_loop(0, parts, last, 0)
        two = pltpu.make_async_copy(a, at1_out, osems.at[1])
        two.start()
        further(tiles)
        further(tiles + 1)
        lax.fori_loop(parts, tiles, ended, 0)
        for k in range(parts):
            move(k, True).wait()
        two.wait()


def forward(x, gate, up, down):
    tokens, d = x.shape
    state = jax.ShapeDtypeStruct((d, tokens), BF16)
    wide, tall = (10, d, TILE), (10, TILE, d)
    return pl.pallas_call(
        forward_kernel,
        grid=(5,),
        in_specs=[ANY] * 4,
        out_specs=[ANY] * 8,
        out_shape=[state] * 4 + [jax.ShapeDtypeStruct(shape, BF16) for shape in (wide, wide, tall)] + [jax.ShapeDtypeStruct((2, 2560, tokens), F32)],
        scratch_shapes=[
            pltpu.VMEM(wide, BF16),
            pltpu.VMEM(wide, BF16),
            pltpu.VMEM(tall, BF16),
            pltpu.VMEM((d, tokens), BF16),
            pltpu.VMEM((d, tokens), F32),
            pltpu.VMEM((TILE, CHUNK), BF16),
            pltpu.VMEM((2, EDGE, d), BF16),
            pltpu.VMEM((2, d, EDGE), BF16),
            pltpu.VMEM((2, CHUNK // SUB, 2, TILE, SUB), F32),
            PAIR,
            PAIR,
            pltpu.SemaphoreType.DMA((10,)),
            pltpu.SemaphoreType.DMA((3, 10)),
            pltpu.SemaphoreType.DMA((4, 10)),
            pltpu.SemaphoreType.DMA((4, 10)),
            PAIR,
            pltpu.SemaphoreType.DMA((2, 2)),
        ],
        compiler_params=pltpu.CompilerParams(
            vmem_limit_bytes=67043328, dimension_semantics=("arbitrary",), collective_id=0, has_side_effects=True
        ),
        cost_estimate=pl.CostEstimate(flops=6 * tokens * d * 2560, bytes_accessed=60 * 2**20, transcendentals=0),
        name="forward_layer",
    )(x, gate, up, down)


class Exchange:
    def __init__(self, jobs, place_of, accs, bufs, outs, ssem, rsem, free, osem):
        self.jobs, self.place_of, self.accs, self.bufs, self.outs = jobs, place_of, accs, bufs, outs
        self.free, self.osem = free, osem
        kept, keep_x, keep_y, send_d, recv_d, send_x, recv_x, send_y, recv_y, done, done_t = bufs
        s, r = lax.axis_index("s"), lax.axis_index("r")
        self.x, self.core = s // 2, s % 2
        self.devices = {"s": s + 1 - 2 * self.core}, {"s": (s + 2) % 4}, {"r": 1 - r}
        self.mine, self.other = pl.ds(pl.multiple_of(r * HALF, HALF), HALF), pl.ds(pl.multiple_of((1 - r) * HALF, HALF), HALF)
        half = done.at[self.mine, :]
        pairs = (send_d, recv_d, 0), (send_x, recv_x, 1), (send_y, recv_y, 2), (half, half, 2)
        self.to = [self.devices[way] for *_, way in pairs]
        self.copies = [
            pltpu.make_async_remote_copy(source, target, ssem.at[i], rsem.at[i], device_id=self.devices[way], device_id_type=MESH)
            for i, (source, target, way) in enumerate(pairs)
        ]

    def meet(self):
        barrier = pltpu.get_barrier_semaphore()
        for device in self.devices:
            pl.semaphore_signal(barrier, 1, device_id=device, device_id_type=MESH)
        return lambda: pl.semaphore_wait(barrier, 3)

    def send(self, number, job):
        @pl.when(job > 0)
        def _():
            pl.semaphore_wait(self.free.at[number], 1)

        self.copies[number].start()

    def arrived(self, number):
        self.copies[number].wait_recv()
        self.copies[number].wait_send()

    def freed(self, number, job):
        @pl.when(job < self.jobs - 1)
        def _():
            pl.semaphore_signal(self.free.at[number], 1, device_id=self.to[number], device_id_type=MESH)

    def pack(self):
        accg, accu, accd = self.accs
        kept, send_d = self.bufs[0], self.bufs[3]

        def cut(owner, ref, slot):
            rows = pl.ds(pl.multiple_of(owner * 224, 32), 224)
            for k in range(4):
                ref[slot, k * 224 : k * 224 + 224, :] = accg[rows, k * 128 : k * 128 + 128].astype(ref.dtype)
                ref[slot, 896 + k * 224 : 1120 + k * 224, :] = accu[rows, k * 128 : k * 128 + 128].astype(ref.dtype)
            ref[slot, 1792:, :] = accd[:, pl.ds(pl.multiple_of(owner * 128, 128), 128)].astype(ref.dtype)

        for slot, place in ((0, self.x), (1, 1 - self.x)):
            cut(2 * place + self.core, kept, slot)
            cut(2 * place + 1 - self.core, send_d, slot)

    def after_partner(self, job):
        kept, keep_x, _, _, recv_d, send_x, *_ = self.bufs
        self.arrived(0)
        send_x[:] = (kept[1] + recv_d[1].astype(F32)).astype(BF16)
        keep_x[:] = kept[0] + recv_d[0].astype(F32)
        self.freed(0, job)
        self.send(1, job)

    def after_across(self, job):
        _, keep_x, keep_y, _, _, _, recv_x, send_y, *_ = self.bufs
        self.arrived(1)
        keep_y[:] = keep_x[self.mine, :] + recv_x[self.mine, :].astype(F32)
        send_y[:] = (keep_x[self.other, :] + recv_x[self.other, :].astype(F32)).astype(BF16)
        self.freed(1, job)
        self.send(2, job)

    def after_beside(self, job):
        keep_y, recv_y, done = self.bufs[2], self.bufs[8], self.bufs[9]
        self.arrived(2)
        done[self.mine, :] = (keep_y[:] + recv_y[:].astype(F32)).astype(BF16)
        self.freed(2, job)
        self.send(3, job)

    def whole(self, job):
        done, done_t = self.bufs[9:]
        self.arrived(3)
        layer, tile = self.place_of(job)
        done_t[:] = done[1792:, :].T
        for i, out in enumerate(self.outs[:2]):
            for k in range(4):
                columns = pl.ds(pl.multiple_of(640 * k + 128 * tile, 128), 128)
                pltpu.make_async_copy(done.at[pl.ds(896 * i + 224 * k, 224), :], out.at[layer, :, columns], self.osem).start()
        pltpu.make_async_copy(done_t, self.outs[2].at[layer, pl.ds(pl.multiple_of(128 * tile, 128), 128), :], self.osem).start()

    def written(self, job):
        done = self.bufs[9]
        pltpu.make_async_copy(done, done, self.osem).wait()
        self.freed(3, job)


EXCHANGE = [
    pltpu.VMEM((2, BLOCK, 128), F32),
    pltpu.VMEM((BLOCK, 128), F32),
    pltpu.VMEM((HALF, 128), F32),
    pltpu.VMEM((2, BLOCK, 128), BF16),
    pltpu.VMEM((2, BLOCK, 128), BF16),
    pltpu.VMEM((BLOCK, 128), BF16),
    pltpu.VMEM((BLOCK, 128), BF16),
    pltpu.VMEM((HALF, 128), BF16),
    pltpu.VMEM((HALF, 128), BF16),
    pltpu.VMEM((BLOCK, 128), BF16),
    pltpu.VMEM((128, 896), BF16),
    pltpu.SemaphoreType.DMA((4,)),
    pltpu.SemaphoreType.DMA((4,)),
    pltpu.SemaphoreType.REGULAR((4,)),
    pltpu.SemaphoreType.DMA,
]


def elementwise(g, u, dp):
    dp = dp.astype(BF16).astype(F32)
    sg = jax.nn.sigmoid(g)
    t = g * sg
    return (t * u).astype(BF16), (dp * u * (sg + t * (1 - sg))).astype(BF16), (dp * t).astype(BF16)


def through_norm(da, h, by):
    da, h = da.astype(BF16).astype(F32), h.astype(F32)
    f = scale_of(h)
    dh = (f * da - h * (f * f * f * jnp.mean(da * h, 0, keepdims=True))).astype(BF16)
    return (by.astype(F32) + dh.astype(F32)).astype(BF16)


def last_kernel(at_in, ht_in, by_in, wg, wu, wd, by_out, og, ou, od, kept_out, sent_out, *refs):
    a, by, total, *accs, p, dg, du, stage, sems, osems = refs[:12]
    ex = Exchange(4, lambda job: (1, job), accs, refs[12:23], (og, ou, od), *refs[23:])
    kept, send_d = ex.bufs[0], ex.bufs[3]
    accg, accu, accd = accs
    n, passes = pl.program_id(0), pl.num_programs(0)
    chunks, steps = a.shape[1] // CHUNK, a.shape[1] // EDGE
    job = n - 1

    @pl.when(n == 0)
    def _():
        met = ex.meet()
        one = pltpu.make_async_copy(at_in, a, osems.at[0])
        one.start()
        met()

        def write(c, t, slot):
            by[:, at(c, EDGE)] = t

        turned(by_in, stage, sems, write)
        total[:] = jnp.zeros_like(total)
        one.wait()

    for acc in accs:
        acc[:] = jnp.zeros_like(acc)

    def step(c, _):
        cols = at(c, CHUNK)
        gate, up, down = wg[:], wu[:], wd[:]
        for i in range(CHUNK // SUB):
            tokens, q = pl.ds(pl.multiple_of(c * CHUNK + i * SUB, SUB), SUB), pl.ds(i * SUB, SUB)
            g, u = dot(gate, a[:, tokens], TN), dot(up, a[:, tokens], TN)
            p[:, q], dg[:, q], du[:, q] = elementwise(g, u, dot(down, by[:, tokens]))
        total[:, cols] += dot(gate, dg[:]) + dot(up, du[:])
        accg[:] += dot(a[:, cols], dg[:], NT)
        accu[:] += dot(a[:, cols], du[:], NT)
        accd[:] += dot(by[:, cols], p[:], NT)

        @pl.when((c == 0) & (job >= 0))
        def _():
            ex.after_partner(job)

        @pl.when((c == 0) & (job >= 1))
        def _():
            ex.whole(job - 1)

        @pl.when((c == 1) & (job >= 1))
        def _():
            ex.written(job - 1)

        @pl.when((c == 2) & (job >= 0))
        def _():
            ex.after_across(job)

        return 0

    lax.fori_loop(0, chunks, step, 0)

    @pl.when(job >= 0)
    def _():
        ex.after_beside(job)

    ex.pack()

    @pl.when(n < passes - 1)
    def _():
        ex.send(0, job + 1)

    @pl.when(n == passes - 1)
    def _():
        one = pltpu.make_async_copy(ht_in, a, osems.at[0])
        one.start()
        three, four = pltpu.make_async_copy(kept, kept_out, sems.at[0]), pltpu.make_async_copy(send_d, sent_out, sems.at[1])
        three.start(), four.start()
        one.wait()

        def last(c, _):
            cols = at(c, EDGE)
            by[:, cols] = through_norm(total[:, cols], a[:, cols], by[:, cols])
            return 0

        lax.fori_loop(0, steps, last, 0)
        two = pltpu.make_async_copy(by, by_out, osems.at[1])
        two.start()
        ex.whole(3)
        ex.written(3)
        three.wait(), four.wait()
        two.wait()


def first_kernel(at_in, ht_in, by_in, gu_in, wg_in, wu_in, wd, kept_in, sent_in, _g, _u, _d, by_out, og, ou, od, dgu_out, *refs):
    a, by, *accs, gu, p, dgu, wgs, wus, dgb, stage, sems, osems, gsem, dsem, lsem, wsem = refs[:18]
    ex = Exchange(6, lambda job: (1 - (job + 4) // 5, (job + 4) % 5), accs, refs[18:29], (og, ou, od), *refs[29:])
    kept, send_d = ex.bufs[0], ex.bufs[3]
    accg, accu, accd = accs
    n, passes = pl.program_id(0), pl.num_programs(0) - 1
    chunks, steps = a.shape[1] // CHUNK, a.shape[1] // EDGE

    def brought(q, slot):
        return pltpu.make_async_copy(gu_in.at[:, at(q // chunks, TILE), at(q % chunks, CHUNK)], gu.at[slot], gsem.at[slot])

    def stored(q, slot):
        return pltpu.make_async_copy(dgu.at[slot], dgu_out.at[:, at(q // chunks, TILE), at(q % chunks, CHUNK)], dsem.at[slot])

    def matrix(tile, i):
        return pltpu.make_async_copy((wg_in, wu_in)[i].at[tile], (wgs, wus)[i].at[:, pl.ds(tile * TILE, TILE)], wsem.at[i, tile])

    @pl.when(n == 0)
    def _():
        met = ex.meet()
        three, four = pltpu.make_async_copy(kept_in, kept, sems.at[0]), pltpu.make_async_copy(sent_in, send_d, sems.at[1])
        three.start(), four.start()
        brought(0, 0).start()
        one, two = pltpu.make_async_copy(at_in, a, osems.at[0]), pltpu.make_async_copy(by_in, by, osems.at[1])
        two.start(), one.start()
        for tile in range(5):
            matrix(tile, 0).start(), matrix(tile, 1).start()
        three.wait(), four.wait()
        met()
        ex.send(0, n)
        two.wait(), one.wait()

    @pl.when(n < passes)
    def _():
        for acc in accs:
            acc[:] = jnp.zeros_like(acc)

        def step(c, _):
            q, slot = n * chunks + c, c % 2
            cols = at(c, CHUNK)
            brought(q, slot).wait()

            @pl.when(q + 1 < passes * chunks)
            def _():
                brought(q + 1, 1 - slot).start()

            @pl.when(q >= 2)
            def _():
                stored(q - 2, slot).wait()

            for i in range(CHUNK // SUB):
                tokens, b = pl.ds(pl.multiple_of(c * CHUNK + i * SUB, SUB), SUB), pl.ds(i * SUB, SUB)
                p[:, b], dgu[slot, 0, :, b], dgu[slot, 1, :, b] = elementwise(gu[slot, 0, :, b], gu[slot, 1, :, b], dot(wd[:], by[:, tokens]))
            accg[:] += dot(a[:, cols], dgu[slot, 0], NT)
            accu[:] += dot(a[:, cols], dgu[slot, 1], NT)
            accd[:] += dot(by[:, cols], p[:], NT)
            stored(q, slot).start()

            @pl.when((c == 0) & (n >= 2))
            def _():
                ex.whole(n - 2)

            @pl.when((c == 0) & (n >= 1))
            def _():
                ex.after_across(n - 1)

            @pl.when(c == 0)
            def _():
                ex.after_partner(n)

            @pl.when((c == 1) & (n >= 2))
            def _():
                ex.written(n - 2)

            @pl.when((c == 2) & (n >= 1))
            def _():
                ex.after_beside(n - 1)

            return 0

        lax.fori_loop(0, chunks, step, 0)
        ex.pack()
        ex.send(0, n + 1)

    @pl.when(n == passes)
    def _():
        one = pltpu.make_async_copy(ht_in, a, osems.at[0])
        one.start()
        for slot in range(2):
            stored(passes * chunks - 2 + slot, slot).wait()

        def brought_back(c, slot):
            return pltpu.make_async_copy(dgu_out.at[:, :, at(c, EDGE)], dgb.at[slot], lsem.at[slot])

        def copy(c, slot):
            return pltpu.make_async_copy(stage.at[slot], by_out.at[at(c, EDGE), :], sems.at[slot])

        brought_back(0, 0).start()
        for tile in range(5):
            matrix(tile, 0).wait(), matrix(tile, 1).wait()
        one.wait()

        def opening():
            ex.whole(3)
            ex.after_across(4)
            ex.after_partner(5)

        hooks = {
            0: opening,
            1: lambda: ex.written(3),
            4: lambda: ex.after_beside(4),
            7: lambda: ex.after_across(5),
            8: lambda: ex.whole(4),
            9: lambda: ex.written(4),
            11: lambda: ex.after_beside(5),
        }

        def step(c, _):
            slot, cols = c % 2, at(c, EDGE)
            brought_back(c, slot).wait()

            @pl.when(c + 1 < steps)
            def _():
                brought_back(c + 1, 1 - slot).start()

            da = dot(wgs[:], dgb[slot, 0]) + dot(wus[:], dgb[slot, 1])

            @pl.when(c >= 2)
            def _():
                copy(c - 2, slot).wait()

            stage[slot] = through_norm(da, a[:, cols], by[:, cols]).T
            copy(c, slot).start()
            for at_step, hook in hooks.items():
                pl.when(c == at_step)(hook)
            return 0

        lax.fori_loop(0, steps, step, 0)
        copy(steps - 2, 0).wait()
        copy(steps - 1, 1).wait()
        ex.whole(5)
        ex.written(5)


def params(number):
    return pltpu.CompilerParams(vmem_limit_bytes=67043328, dimension_semantics=("arbitrary",), collective_id=number, has_side_effects=True)


def gradients():
    return [jax.ShapeDtypeStruct(shape, BF16) for shape in ((2, 224, 2560), (2, 224, 2560), (2, 640, 896))]


def backward_last(a, h, by, weights):
    d, tokens = a.shape
    return pl.pallas_call(
        last_kernel,
        grid=(5,),
        in_specs=[ANY, ANY, ANY] + [pl.BlockSpec((None, *w.shape[1:]), lambda n: (5 + n, 0, 0)) for w in weights],
        out_specs=[ANY] * 6,
        out_shape=[jax.ShapeDtypeStruct((d, tokens), BF16), *gradients(), jax.ShapeDtypeStruct((2, BLOCK, 128), F32), jax.ShapeDtypeStruct((2, BLOCK, 128), BF16)],
        scratch_shapes=[
            pltpu.VMEM((d, tokens), BF16),
            pltpu.VMEM((d, tokens), BF16),
            pltpu.VMEM((d, tokens), F32),
            *[pltpu.VMEM((d, TILE), F32)] * 3,
            *[pltpu.VMEM((TILE, CHUNK), BF16)] * 3,
            pltpu.VMEM((2, EDGE, d), BF16),
            PAIR,
            PAIR,
            *EXCHANGE,
        ],
        compiler_params=params(1),
        cost_estimate=pl.CostEstimate(flops=16 * tokens * d * 2560, bytes_accessed=60 * 2**20, transcendentals=0),
        name="backward_last",
    )(a, h, by, *weights)


def backward_first(a, h, by, gu, weights, kept, sent, sums):
    d, tokens = a.shape
    return pl.pallas_call(
        first_kernel,
        grid=(6,),
        in_specs=[ANY] * 6 + [pl.BlockSpec((None, TILE, d), lambda n: (n - n // 5, 0, 0))] + [ANY] * 5,
        out_specs=[ANY] * 5,
        out_shape=[jax.ShapeDtypeStruct((tokens, d), BF16), *gradients(), jax.ShapeDtypeStruct((2, 2560, tokens), BF16)],
        input_output_aliases={9: 1, 10: 2, 11: 3},
        scratch_shapes=[
            pltpu.VMEM((d, tokens), BF16),
            pltpu.VMEM((d, tokens), BF16),
            *[pltpu.VMEM((d, TILE), F32)] * 3,
            pltpu.VMEM((2, 2, TILE, CHUNK), F32),
            pltpu.VMEM((TILE, CHUNK), BF16),
            pltpu.VMEM((2, 2, TILE, CHUNK), BF16),
            pltpu.VMEM((d, 2560), BF16),
            pltpu.VMEM((d, 2560), BF16),
            pltpu.VMEM((2, 2, 2560, EDGE), BF16),
            pltpu.VMEM((2, EDGE, d), BF16),
            PAIR,
            PAIR,
            PAIR,
            PAIR,
            PAIR,
            pltpu.SemaphoreType.DMA((2, 5)),
            *EXCHANGE,
        ],
        compiler_params=params(2),
        cost_estimate=pl.CostEstimate(flops=12 * tokens * d * 2560, bytes_accessed=200 * 2**20, transcendentals=0),
        name="backward_first",
    )(a, h, by, gu, *weights, kept, sent, *sums)


def solution(mesh):
    def step(x, dy, *weights):
        xt, a0, h1, a1, *whole, gu = forward(x[0], *weights)
        by_h1, *sums, kept, sent = backward_last(a1, h1, dy[0], whole)
        by_x, *sums, _ = backward_first(a0, xt, by_h1, gu, whole, kept, sent, sums)
        return by_x[None], *sums

    states, cut = P(("rep", "r", "s"), None, None), P(None, "s", None)
    return jax.shard_map(
        step,
        mesh=mesh,
        in_specs=(states, states) + (cut,) * 3,
        out_specs=(states,) + (P("rep", "s", None),) * 3,
        check_vma=False,
    )
```

time: 1070 us -> 522 us (0.49)
  waiting for transfers between devices: 539 us -> 0 us
  between operations: 14 us -> 0.68 us
    reduce_scatter x6 -> x0, waiting for transfers between devices: 254 us -> none  [summed(): lax.psum_scatter(term, 's', scatter_dimension=0, tiled=True)]
    psum x1 -> x0, waiting for transfers between devices: 163 us -> none  [summed(): lax.psum(lax.psum_scatter(term, 's', scatter_dimension=0, tiled=True), 'r')]
    all_gather x6 -> x0, waiting for transfers between devices: 118 us -> none  [fetched(): return [lax.all_gather(w[number], 's', axis=0, tiled=True) for w in weights]]
    unnamed x10, local copies, waits for them, and re-layouts: 0.02 us -> 11 us
  transfers between devices with their start and end apart: 13 -> 0, of which waited for: 11 -> 0; matrix products, arithmetic and copies ran while one was open for 0% -> 0% of each run, Pallas kernels for 8% -> 0%
where the time goes in v3:
time: 522 us
  Pallas kernels  510 us (98%)
  local copies, waits for them, and re-layouts  11 us (2%)
    pallas_call x1, Pallas kernels, backward_last(): pl.pallas_call(last_kernel, grid=(5,), in_specs=[ANY, ANY, ANY] + [pl.Blo...  214 us
    pallas_call x1, Pallas kernels, backward_first(): pl.pallas_call(first_kernel, grid=(6,), in_specs=[ANY] * 6 + [pl.BlockSpe...  174 us
    pallas_call x1, Pallas kernels, forward(): pl.pallas_call(forward_kernel, grid=(5,), in_specs=[ANY] * 4, out_specs=[...  122 us
    unnamed x10, local copies, waits for them, and re-layouts  11 us

profile of v3, /device:TPU:0, one launch (start us, length us, event | category | flops | bytes accessed | tf_op | source)
XLA Modules:
  0.0 521.8 jit_solution(10831805378544239839)
XLA Ops:
  0.6 122.4 %forward_layer.1 = (bf16[896,4096]{1,0:T(8,128)(2,1)}, bf16[896,4096]{1,0:T(8,128)(2,1)}, bf16[896,4096]{1,0:T(8,128)(2,1)}, bf16[896,4096]{1,0:T(8,128)(2,1)}, ...) custom-call(bf16[4096,896]{1,0:T(8,128)(2,1)} %bitcast.4, ...), custom_call_target="tpu_custom_call" | custom-call | flops 56371445760 | bytes 62914560 | tf_op jit(solution)/shard_map/forward_layer/pallas_call | solution.py:231
  123.0 214.1 %backward_last.1 = (bf16[896,4096]{1,0:T(8,128)(2,1)}, bf16[2,224,2560]{2,1,0:T(8,128)(2,1)}, bf16[2,224,2560]{2,1,0:T(8,128)(2,1)}, bf16[2,640,896]{2,1,0:T(8,1...) custom-call(bf16[896,4096]{1,0:T(8,128)(2,1)} %get-tuple-element.24.at_in, ...), custom_call_target="tpu_custom_call" | custom-call | flops 150323855360 | bytes 62914560 | tf_op jit(solution)/shard_map/backward_last/pallas_call | solution.py:635
  337.2 173.5 %backward_first.1 = (bf16[4096,896]{1,0:T(8,128)(2,1)}, bf16[2,224,2560]{2,1,0:T(8,128)(2,1)}, bf16[2,224,2560]{2,1,0:T(8,128)(2,1)}, bf16[2,640,896]{2,1,0:T(8,128)(2,1)}, bf16[2,2560,4096]{2,1,0:T(8,128)(2,1)}) custom-call(bf16[896,4096]{1,0:T(8,128)(2,1)} %get-tuple-element.22.at_in, ...), custom_call_target="tpu_custom_call", output_to_operand_aliasing={{1}: (9, {}), {2}: (10, {}), {3}: (11, {})} | custom-call | flops 112742891520 | bytes 209715200 | tf_op jit(solution)/shard_map/backward_first/pallas_call | solution.py:660
  510.7 0.0 copy-start
  510.7 0.0 copy-start.1
  510.7 6.9 %copy.19 = bf16[1,4096,896]{2,1,0:T(8,128)(2,1)} copy(bf16[1,4096,896]{2,1,0:T(8,128)(2,1)} %bitcast.3) | data formatting | bytes 14680064
  517.6 0.0 copy-done
  517.6 0.0 copy-start.2
  517.6 1.4 copy.20
  519.0 0.0 copy-done.1
  519.0 1.4 copy.21
  520.4 0.0 copy-done.2
  520.4 1.4 copy.22
Async XLA Ops:
  510.7 6.9 %copy-start = (bf16[2,224,2560]{2,1,0:T(8,128)(2,1)S(1)}, bf16[2,224,2560]{2,1,0:T(8,128)(2,1)}, u32[]{:S(2)}) copy-start(bf16[2,224,2560]{2,1,0:T(8,128)(2,1)} %get-tuple-element.45) | copy-start | bytes 6881284
  510.7 8.3 %copy-start.1 = (bf16[2,224,2560]{2,1,0:T(8,128)(2,1)S(1)}, bf16[2,224,2560]{2,1,0:T(8,128)(2,1)}, u32[]{:S(2)}) copy-start(bf16[2,224,2560]{2,1,0:T(8,128)(2,1)} %get-tuple-element.46) | copy-start | bytes 6881284
  517.6 2.8 copy-start.2
